TPU v7x, 32 devices: a whole 2x2x4 slice. The times are simulated.
32 devices in a mesh: grp: 2 (over x), blk: 8 (over z, y), vec: 2 (over core).
Axes of the slice: x: 2, y: 2, z: 4, core: 2. Of those that a mesh axis runs over, the one named last changes fastest.
Arguments:
- trial: bfloat16 [20480, 32], P(('grp', 'blk', 'vec')), may hold values from -6 to 6
- energy_gap: float32 [20480], P(('grp', 'blk', 'vec')), may hold values from 0.5 to 2.5
- coulomb_factors: bfloat16 [4096, 20480], P('blk'), may hold values from -0.0390625 to 0.0390625
- occ_values: bfloat16 [80, 40, 512], P('blk'), may hold values from -1 to 1
- vir_values: bfloat16 [80, 512, 512], P('blk'), may hold values from -1 to 1
- kernel: float32 [80, 512], P('blk'), may hold values from 0.2 to 2
- live_points: int32 [80], P('blk'), may hold values from 64 to 512
Outputs:
- sigma: bfloat16 [20480, 32], P(('grp', 'blk', 'vec'))
All inputs are finite; a program needn't handle non-finite values.
Results may differ from a plain program's by a relative error of at most 0.0029.
Values may be sent and summed in bfloat16 or wider, within the bound.
No kernel may reach another device: no remote copies, remote signals or barrier semaphores. Data moves between devices by JAX's collectives and lax.ppermute only.
A program may use at most 64 MiB of HBM per device.

v0:
```python
import jax
import jax.numpy as jnp
from jax import lax
from jax.experimental import pallas as pl
from jax.experimental.pallas import tpu as pltpu
from jax.sharding import PartitionSpec as P


LANES = 128
HEAD = 10**10
NT = (((1,), (1,)), ((), ()))
NN = (((1,), (0,)), ((), ()))
VMEM = pl.BlockSpec(memory_space=pltpu.VMEM)
SMEM = pl.BlockSpec(memory_space=pltpu.SMEM)
ANY = pl.BlockSpec(memory_space=pl.ANY)


def digits_of(count):
    digits, stride = [], 1
    bits = count.bit_length() - 1
    if bits % 2:
        digits.append((1, 2))
        stride = 2
    while stride < count:
        digits.append((stride, 4))
        stride *= 4
    return digits


def swap(x, axis, count, mask):
    return lax.ppermute(x, axis, [(i, i ^ mask) for i in range(count)])


def call(body, out_shape, in_specs, flops=0, scratch=(), limit=14):
    return pl.pallas_call(
        body,
        out_shape=out_shape,
        in_specs=in_specs,
        out_specs=jax.tree.map(lambda _: VMEM, out_shape),
        scratch_shapes=list(scratch),
        compiler_params=pltpu.CompilerParams(vmem_limit_bytes=limit * 2**20),
        cost_estimate=pl.CostEstimate(flops=flops, bytes_accessed=0, transcendentals=0),
    )


def after(body, count):
    return lambda *refs: body(*refs[:count], *refs[count + 1 :])


def shape(dims, dtype):
    return jax.ShapeDtypeStruct(dims, dtype)


class Plan:
    def __init__(self, sizes, trial, coulomb_factors, occ_values, vir_values):
        self.groups, self.blks, self.vecs = sizes
        self.rows, self.k = trial.shape
        self.aux = coulomb_factors.shape[0] // self.vecs
        self.pairs = coulomb_factors.shape[1] // self.groups
        self.batches = occ_values.shape[0] // self.vecs
        self.occ_all, self.points = occ_values.shape[1:]
        self.occs = self.occ_all // self.groups
        self.virs = vir_values.shape[2]
        self.aligned = self.rows % LANES == 0
        self.count = self.blks if self.aligned else 1
        self.length = self.rows if self.aligned else self.pairs // self.vecs
        self.per = self.length // LANES
        self.digits = digits_of(self.blks)
        stride, radix = self.digits[-1]
        self.top = stride
        if self.aligned and radix == 4 and len(self.digits) == 2 and self.occs % radix == 0:
            self.parts = [(2, 3), (0, 1)]
            self.run = self.occs // radix
        else:
            assert not self.aligned
            self.parts = [(0,)]
            self.run = self.occs

        if 2 * self.aux <= self.points and self.aux % LANES == 0:
            self.packed = [(0, 0), (0, self.aux)]
        else:
            self.packed = [(0, 0), (1, 0)]
        self.slots = self.packed[-1][0] + 1

    def masks(self, part):
        if len(self.parts) == 1:
            return list(range(self.count))
        return [d * self.top + low for d in part for low in range(self.top)]

    def first_row(self, d):
        return (lax.axis_index("blk") // self.top ^ d) * self.run if len(self.parts) > 1 else 0

    def owner(self, m):
        return lax.axis_index("blk") ^ m if self.aligned else 0

    def part(self, h):
        return lax.axis_index("vec") ^ h if self.aligned else h

    def block(self, h, m, j):
        return (self.owner(m) * self.vecs + self.part(h)) * self.per + j

    def place(self, h, m, j):
        at = self.block(h, m, j)
        tiles = self.virs // LANES
        return (
            pl.ds(pl.multiple_of((at // tiles) * self.k, self.k), self.k),
            pl.ds(pl.multiple_of((at % tiles) * LANES, LANES), LANES),
        )


def copy_kernel(plan, given, out):
    out[...] = given[...]


def stack_kernel(plan, *refs):
    for m, piece in enumerate(refs[:-1]):
        refs[-1][m] = piece[...]


def occ_rows(plan, occ, b, occ32):
    occ32[...] = occ[lax.axis_index("vec") * plan.batches + b].astype(jnp.float32)
    base = lax.axis_index("grp") * plan.occs
    return lambda i: occ32[pl.ds(base + i, 1), :]


def factor_block(plan, fac, m, p):
    top = pl.multiple_of(lax.axis_index("vec") * plan.aux, plan.aux)
    at = lax.axis_index("grp") * plan.pairs + (plan.owner(m) * plan.vecs + p) * plan.length
    return fac[pl.ds(top, plan.aux), pl.ds(pl.multiple_of(at, LANES), plan.length)]


def rows_kernel(plan, mine, other, rows):
    for h, half in enumerate((mine, other)):
        for m in range(plan.count):
            for j in range(plan.per):
                rows[plan.place(h, m, j)] = half[m, :, j * LANES : (j + 1) * LANES]


def dens_kernel(plan, span, rows, vir, occ, dens, sent, occ32):
    k = plan.k
    vec = lax.axis_index("vec")
    for n, b in enumerate(span):
        row = occ_rows(plan, occ, b, occ32.at[n])
        trans = lax.dot_general(
            rows[...], vir[vec * plan.batches + b], NT, preferred_element_type=jnp.float32
        )
        total = row(0) * trans[:k, :]
        for i in range(1, plan.occs):
            total = total + row(i) * trans[i * k : (i + 1) * k, :]
        dens[n] = total
        sent[n] = total.astype(sent.dtype)


def first_dens_kernel(plan, span, mine, other, vir, occ, dens, sent, rows, occ32):
    rows_kernel(plan, mine, other, rows)
    dens_kernel(plan, span, rows, vir, occ, dens, sent, occ32)


def fac_kernel(plan, h, half, fac, *refs):
    value = refs[0][...] if len(refs) > 1 else 0.0
    for m in range(plan.count):
        value += lax.dot_general(
            half[m], factor_block(plan, fac, m, plan.part(h)), NT, preferred_element_type=jnp.float32
        )
    refs[-1][...] = value


def second_dens_kernel(plan, span, rows, vir, occ, other, fac, part, dens, sent, total, occ32):
    dens_kernel(plan, span, rows, vir, occ, dens, sent, occ32)
    fac_kernel(plan, 1, other, fac, part, total)
    value = total[...]
    if 2 * plan.aux < plan.slots * plan.points:
        for slot in range(plan.slots):
            sent[len(span) + slot] = jnp.zeros(sent.shape[1:], sent.dtype)
    for slot, lane in plan.packed:
        term = value.astype(sent.dtype)
        sent[len(span) + slot, :, lane : lane + plan.aux] = term
        value = value - term.astype(jnp.float32)


def grid_kernel(plan, part, span, skip, live, dens_a, dens_b, occ, weight, vir, *refs):
    acc, scaled, occ32 = refs[-3:]
    k = plan.k
    base = lax.axis_index("vec") * plan.batches
    slots = lax.broadcasted_iota(jnp.int32, (1, plan.points), 1)
    for n, b in enumerate(span):
        row = occ_rows(plan, occ, b, occ32.at[n])
        density = dens_a[n] + dens_b[n].astype(jnp.float32)
        used = jnp.where(slots < live[base + b], weight[pl.ds(base + b, 1), :], 0.0)
        weighted = density * used
        for t, d in enumerate(part):
            first = plan.first_row(d)
            for r in range(plan.run):
                at = (t * plan.run + r) * k
                scaled[at : at + k, :] = (row(first + r) * weighted).astype(jnp.bfloat16)
        value = lax.dot_general(scaled[...], vir[base + b], NN, preferred_element_type=jnp.float32)
        if n:
            acc[...] += value
        elif skip is None:
            acc[...] = value
        else:
            acc[...] = refs[0][pl.ds(skip, acc.shape[0]), :] + value


def back_kernel(plan, part, part_a, part_b, fac, acc, stay, sent):
    both = part_a[...]
    first = part_b.shape[0] - plan.slots
    for slot, lane in plan.packed:
        both = both + part_b[first + slot, :, lane : lane + plan.aux].astype(jnp.float32)
    both = both.astype(jnp.bfloat16)
    k, tiles = plan.k, plan.virs // LANES
    masks = plan.masks(part)
    for n, m in enumerate(masks):
        t = n * len(part) // len(masks)
        first = plan.first_row(part[t])
        for h, out in enumerate((stay, sent)):
            value = 2.0 * lax.dot_general(
                both,
                factor_block(plan, fac, m, plan.part(h)),
                NN,
                preferred_element_type=jnp.float32,
            )
            for j in range(plan.per):
                at = plan.block(h, m, j)
                row = (at // tiles - first + t * plan.run) * k
                found = acc[
                    pl.ds(pl.multiple_of(row, k), k),
                    pl.ds(pl.multiple_of((at % tiles) * LANES, LANES), LANES),
                ]
                lanes = slice(j * LANES, (j + 1) * LANES)
                out[n, :, lanes] = (value[:, lanes] + found).astype(out.dtype)


def sum_kernel(plan, radix, stay, came, *outs):
    for n in range(stay.shape[0]):
        out = outs[n % radix]
        out[n // radix] = (stay[n] + came[n].astype(jnp.float32)).astype(out.dtype)


def split_kernel(plan, own, *refs):
    outs = refs[-own.shape[0] :]
    for n, out in enumerate(outs):
        total = own[n]
        for came in refs[: -len(outs)]:
            total = total + came[n].astype(jnp.float32)
        out[...] = total.astype(out.dtype)


def local(trial, energy_gap, coulomb_factors, occ_values, vir_values, kernel, live_points, sizes):
    plan = Plan(sizes, trial, coulomb_factors, occ_values, vir_values)
    groups, blks, vecs, k = plan.groups, plan.blks, plan.vecs, plan.k
    batches, points, virs, occs = plan.batches, plan.points, plan.virs, plan.occs
    digits = plan.digits
    half = (plan.count, k, plan.length)
    bf16, f32 = jnp.bfloat16, jnp.float32

    def bind(body, *first):
        return lambda *refs: body(plan, *first, *refs)

    trial_cols = trial.T
    pieces, masks = [trial_cols], [0]
    for stride, radix in reversed(digits):
        known = len(masks)
        for d in range(1, radix):
            for n in range(known):
                pieces.append(swap(pieces[n], "blk", blks, d * stride))
                masks.append(masks[n] ^ (d * stride))
        if known == 1:
            pieces[-1] = call(
                bind(copy_kernel), shape(trial_cols.shape, bf16), [VMEM], flops=HEAD
            )(pieces[-1])
    pieces = [p for _, p in sorted(zip(masks, pieces), key=lambda pair: pair[0])]

    if plan.aligned:
        mine = call(
            after(bind(stack_kernel), 0), shape(half, bf16), [VMEM] * (len(pieces) + 1)
        )(vir_values, *pieces)
        other = swap(mine, "vec", vecs, 1)
    else:
        me, vec = lax.axis_index("blk"), lax.axis_index("vec")
        mine = jnp.take(jnp.stack(pieces), me ^ jnp.arange(blks), axis=0)
        both = jnp.stack([mine, swap(mine, "vec", vecs, 1)])
        both = jnp.take(both, vec ^ jnp.arange(vecs), axis=0)
        both = both.transpose(2, 1, 0, 3).reshape(k, vecs, plan.length)
        mine, other = both[None, :, 0], both[None, :, 1]

    flops = k * plan.aux * plan.pairs
    part = call(bind(fac_kernel, 0), shape((k, plan.aux), f32), [VMEM] * 2, flops)(
        mine, coulomb_factors
    )

    cut = (batches + 1) // 2
    spans = [tuple(range(cut)), tuple(range(cut, batches))]
    chunks = [(len(span), k, points) for span in spans]
    grid_flops = 2 * points * virs * occs * k

    def occ_scratch(span):
        return pltpu.VMEM((len(span), plan.occ_all, points), f32)

    first_dens, sent, rows = call(
        after(bind(first_dens_kernel, spans[0]), 4),
        (shape(chunks[0], f32), shape(chunks[0], bf16), shape((occs * k, virs), bf16)),
        [VMEM] * 4 + [ANY],
        grid_flops * len(spans[0]),
        [occ_scratch(spans[0])],
    )(mine, other, vir_values, occ_values, part)
    first_other = swap(sent, "grp", groups, 1)
    second_dens, sent, part = call(
        bind(second_dens_kernel, spans[1]),
        (
            shape(chunks[1], f32),
            shape((len(spans[1]) + plan.slots, k, points), bf16),
            shape((k, plan.aux), f32),
        ),
        [VMEM] * 6,
        grid_flops * len(spans[1]) + flops,
        [occ_scratch(spans[1])],
    )(rows, vir_values, occ_values, other, coulomb_factors, part)
    second_other = swap(sent, "grp", groups, 1)

    def grid(chosen, chunk, dens, came, skip, *more):
        used = plan.run * len(chosen)
        count = 6 + (skip is not None)
        body = bind(grid_kernel, chosen, spans[chunk], skip)
        return call(
            after(body, count) if len(more) + 6 > count else body,
            shape((used * k, virs), f32),
            [SMEM] + [VMEM] * (count - 1) + [ANY] * (len(more) + 6 - count),
            grid_flops * len(spans[chunk]) * used // occs,
            [pltpu.VMEM((used * k, points), bf16), occ_scratch(spans[chunk])],
        )(live_points, dens, came, occ_values, kernel, vir_values, *more)

    every = sum(plan.parts, ())
    begun = grid(every, 0, first_dens, first_other, None, sent)

    def finish(number, *order):
        skip = sum(len(chosen) for chosen in plan.parts[:number]) * plan.run * k
        return grid(plan.parts[number], 1, second_dens, second_other, skip, begun, *order)

    def back(number, acc, *order):
        chosen = plan.parts[number]
        share = (len(plan.masks(chosen)),) + half[1:]
        body = bind(back_kernel, chosen)
        return call(
            after(body, 4) if order else body,
            (shape(share, f32), shape(share, bf16)),
            [VMEM] * 4 + [ANY] * len(order),
            2 * flops // len(plan.parts),
        )(part, second_other, coulomb_factors, acc, *order)

    if len(plan.parts) == 2:
        (stride, radix), (top, _) = digits
        count = plan.count // 2

        def first_sum(stay, sent, *order):
            body = bind(sum_kernel, radix)
            return call(
                after(body, 2) if order else body,
                (shape((count // radix,) + half[1:], f32),)
                + (shape((count // radix,) + half[1:], bf16),) * (radix - 1),
                [VMEM] * 2 + [ANY] * len(order),
            )(stay, swap(sent, "vec", vecs, 1), *order)

        def next_sum(number, own, sends):
            came = [swap(x, "blk", blks, (d + 1) * stride) for d, x in enumerate(sends)]
            out = [shape(half[1:], bf16 if d else f32) for d in plan.parts[number]]
            outs = call(bind(split_kernel), out, [VMEM] * (1 + len(came)))(own, *came)
            return [
                swap(x, "blk", blks, d * top) if d else x
                for d, x in zip(plan.parts[number], outs)
            ]

        stay, sent = back(0, finish(0))
        acc = finish(1, stay)
        far = first_sum(stay, sent, acc)
        stay, sent = back(1, acc, far[0])
        near = first_sum(stay, sent)
        came = next_sum(0, far[0], far[1:]) + next_sum(1, near[0], near[1:])
    else:
        stay, sent = back(0, finish(0))
        full = jnp.concatenate([stay[0], sent[0].astype(f32)], axis=1)
        full = full.reshape(k, blks, vecs, plan.rows).transpose(2, 1, 0, 3)
        full = jnp.take(full, me ^ jnp.arange(blks), axis=1)
        full = jnp.take(full, vec ^ jnp.arange(vecs), axis=0)
        total = full[0] + swap(full[1].astype(bf16), "vec", vecs, 1).astype(f32)
        for stride, radix in digits:
            total = total.reshape((-1, radix) + total.shape[1:])
            total = sum(
                (
                    swap(total[:, d].astype(bf16), "blk", blks, d * stride).astype(f32)
                    for d in range(1, radix)
                ),
                total[:, 0],
            )
        came = [total[0]]
    total = sum((x.astype(f32) for x in came[1:]), came[0].astype(f32))
    result = energy_gap[None, :] * trial_cols.astype(f32) + total
    return result.astype(bf16).T


def solution(mesh):
    sizes = tuple(mesh.shape[a] for a in ("grp", "blk", "vec"))
    in_specs = (
        P(("grp", "blk", "vec"), None),
        P(("grp", "blk", "vec")),
        P("blk", None),
        P("blk", None, None),
        P("blk", None, None),
        P("blk", None),
        P("blk"),
    )
    out_specs = P(("grp", "blk", "vec"), None)

    def program(*args):
        return local(*args, sizes=sizes)

    return jax.shard_map(
        program, mesh=mesh, in_specs=in_specs, out_specs=out_specs, check_vma=False
    )
```

profile of v0, /device:TPU:0, one launch (start us, length us, event | category | flops | bytes accessed | tf_op | source)
XLA Modules:
  0.0 43.6 jit_solution(14827458879440219744)
XLA Ops:
  0.0 0.0 slice-start.5
  0.0 0.0 slice-start
  0.0 0.0 slice-start.6
  0.0 0.0 copy-start.2
  0.0 0.0 slice-start.2
  0.0 0.0 slice-start.3
  0.0 0.0 slice-start.4
  0.0 5.2 %collective-permute-start.5 = (bf16[32,640]{1,0:T(8,128)(2,1)}, bf16[32,640]{1,0:T(8,128)(2,1)S(1)}, u32[]{:S(2)}, u32[]{:S(2)}) collective-permute-start(bf16[32,640]{1,0:T(8,128)(2,1)} %bitcast.8), channel_id=1, source_target_pairs={{0,12},{2,14},{4,8},{6,10},{8,4},{10,6},{12,0},{14,2},{1,13},{3,15... | collective-permute-start | bytes 122888 | tf_op jit(solution)/shard_map/ppermute | solution.py:31
  5.2 0.0 collective-permute-start.3
  5.2 0.6 %collective-permute-start.1 = (bf16[32,640]{1,0:T(8,128)(2,1)}, bf16[32,640]{1,0:T(8,128)(2,1)S(1)}, u32[]{:S(2)}, u32[]{:S(2)}) collective-permute-start(bf16[32,640]{1,0:T(8,128)(2,1)} %bitcast.10), channel_id=1, source_target_pairs={{0,4},{2,6},{4,0},{6,2},{8,12},{10,14},{12,8},{14,10},{1,5},{3,7},... | collective-permute-start | bytes 122888 | tf_op jit(solution)/shard_map/ppermute | solution.py:31
  5.8 1.7 %collective-permute-start = (bf16[32,640]{1,0:T(8,128)(2,1)}, bf16[32,640]{1,0:T(8,128)(2,1)S(1)}, u32[]{:S(2)}, u32[]{:S(2)}) collective-permute-start(bf16[32,640]{1,0:T(8,128)(2,1)} %bitcast.11), channel_id=1, source_target_pairs={{0,2},{2,0},{4,6},{6,4},{8,10},{10,8},{12,14},{14,12},{1,3},{3,1},... | collective-permute-start | bytes 122888 | tf_op jit(solution)/shard_map/ppermute | solution.py:31
  7.5 0.0 collective-permute-done.5.refs_0_
  7.5 1.8 %collective-permute-start.6 = (bf16[32,640]{1,0:T(8,128)(2,1)S(1)}, bf16[32,640]{1,0:T(8,128)(2,1)S(1)}, u32[]{:S(2)}, u32[]{:S(2)}) collective-permute-start(bf16[32,640]{1,0:T(8,128)(2,1)S(1)} %shard_map.73.refs_7_), channel_id=1, source_target_pairs={{0,2},{2,0},{4,6},{6,4},{8,10},{10,8},{12,14},{14,12},{1,3},{3,1},... | collective-permute-start | bytes 122888 | tf_op jit(solution)/shard_map/ppermute | solution.py:31
  9.3 1.0 %collective-permute-done.3.refs_5_ = bf16[32,640]{1,0:T(8,128)(2,1)S(1)} collective-permute-done((bf16[32,640]{1,0:T(8,128)(2,1)}, bf16[32,640]{1,0:T(8,128)(2,1)S(1)}, u32[]{:S(2)}, u32[]{:S(2)}) %collective-permute-start.3) | collective-permute-done | bytes 40992 | tf_op jit(solution)/shard_map/ppermute | solution.py:31
  10.3 1.5 %collective-permute-start.4 = (bf16[32,640]{1,0:T(8,128)(2,1)S(1)}, bf16[32,640]{1,0:T(8,128)(2,1)S(1)}, u32[]{:S(2)}, u32[]{:S(2)}) collective-permute-start(bf16[32,640]{1,0:T(8,128)(2,1)S(1)} %collective-permute-done.3.refs_5_), channel_id=1, source_target_pairs={{0,2},{2,0},{4,6},{6,4},{8,10},{10,8},{12,14},{14,12},{1,3},{3,1},... | collective-permute-start | bytes 122888 | tf_op jit(solution)/shard_map/ppermute | solution.py:31
  11.8 0.0 collective-permute-done.1.refs_3_
  11.8 0.5 %collective-permute-start.2 = (bf16[32,640]{1,0:T(8,128)(2,1)S(1)}, bf16[32,640]{1,0:T(8,128)(2,1)S(1)}, u32[]{:S(2)}, u32[]{:S(2)}) collective-permute-start(bf16[32,640]{1,0:T(8,128)(2,1)S(1)} %collective-permute-done.1.refs_3_), channel_id=1, source_target_pairs={{0,2},{2,0},{4,6},{6,4},{8,10},{10,8},{12,14},{14,12},{1,3},{3,1},... | collective-permute-start | bytes 122888 | tf_op jit(solution)/shard_map/ppermute | solution.py:31
  12.3 0.0 collective-permute-done.refs_2_
  12.4 0.0 collective-permute-done.6.refs_8_
  12.4 2.0 %collective-permute-done.4.refs_6_ = bf16[32,640]{1,0:T(8,128)(2,1)S(1)} collective-permute-done((bf16[32,640]{1,0:T(8,128)(2,1)S(1)}, bf16[32,640]{1,0:T(8,128)(2,1)S(1)}, u32[]{:S(2)}, u32[]{:S(2)}) %collective-permute-start.4) | collective-permute-done | bytes 40992 | tf_op jit(solution)/shard_map/ppermute | solution.py:31
  14.3 1.5 %collective-permute-done.2.refs_4_ = bf16[32,640]{1,0:T(8,128)(2,1)S(1)} collective-permute-done((bf16[32,640]{1,0:T(8,128)(2,1)S(1)}, bf16[32,640]{1,0:T(8,128)(2,1)S(1)}, u32[]{:S(2)}, u32[]{:S(2)}) %collective-permute-start.2) | collective-permute-done | bytes 40992 | tf_op jit(solution)/shard_map/ppermute | solution.py:31
  15.8 0.0 slice-done.5
  15.8 0.0 slice-done.6
  15.8 0.0 copy-done.2
  15.9 0.0 copy-start
  15.9 0.1 collective-permute-start.7
  16.0 0.0 slice-done
  16.0 0.0 slice-done.1
  16.0 0.0 slice-done.2
  16.0 0.0 slice-done.3
  16.0 0.0 slice-done.4
  16.0 0.9 %shard_map.75.refs_4_.refs_5_ = f32[32,256]{1,0:T(8,128)S(1)} custom-call(bf16[8,32,640]{2,1,0:T(8,128)(2,1)S(1)} %shard_map.74.refs_0_, bf16[512,20480]{1,0:T(8,128)(2,1)S(1)} %bitcast.5), custom_call_target="tpu_custom_call" | custom-call | flops 83886080 | tf_op jit(solution)/shard_map/pallas_call | solution.py:288
  16.9 0.7 %collective-permute-done.7.refs_1_.refs_3_ = bf16[8,32,640]{2,1,0:T(8,128)(2,1)S(1)} collective-permute-done((bf16[8,32,640]{2,1,0:T(8,128)(2,1)S(1)}, bf16[8,32,640]{2,1,0:T(8,128)(2,1)S(1)}, u32[]{:S(2)}, u32[]{:S(2)}) %collective-permute-start.7) | collective-permute-done | bytes 327712 | tf_op jit(solution)/shard_map/ppermute | solution.py:31
  17.6 0.0 copy-done
  17.6 1.8 %shard_map.76 = (f32[3,32,512]{2,1,0:T(8,128)S(1)}, bf16[3,32,512]{2,1,0:T(8,128)(2,1)S(1)}, bf16[640,512]{1,0:T(8,128)(2,1)S(1)}) custom-call(bf16[8,32,640]{2,1,0:T(8,128)(2,1)S(1)} %shard_map.74.refs_0_, bf16[8,32,640]{2,1,0:T(8,128)(2,1)S(1)} %collective-permute-done.7.refs_1_.refs_3_, bf16[10,512,512]{2,1,0:T(8,128)(2,1)S(1)} %bitcast.7, ...), custom_call_target="tpu_custom_call" | custom-call | flops 1006632960 | tf_op jit(solution)/shard_map/pallas_call | solution.py:300
  19.4 1.6 %collective-permute-start.9 = (bf16[3,32,512]{2,1,0:T(8,128)(2,1)S(1)}, bf16[3,32,512]{2,1,0:T(8,128)(2,1)S(1)}, u32[]{:S(2)}, u32[]{:S(2)}) collective-permute-start(bf16[3,32,512]{2,1,0:T(8,128)(2,1)S(1)} %get-tuple-element.28), channel_id=1, source_target_pairs={{0,16},{16,0},{1,17},{17,1},{2,18},{18,2},{3,19},{19,3},{4,20},{20... | collective-permute-start | bytes 294920 | tf_op jit(solution)/shard_map/ppermute | solution.py:31
  21.0 1.6 %shard_map.77 = (f32[2,32,512]{2,1,0:T(8,128)S(1)}, bf16[3,32,512]{2,1,0:T(8,128)(2,1)S(1)}, f32[32,256]{1,0:T(8,128)S(1)}) custom-call(bf16[640,512]{1,0:T(8,128)(2,1)S(1)} %get-tuple-element.23.refs_0_, bf16[10,512,512]{2,1,0:T(8,128)(2,1)S(1)} %bitcast.7, bf16[10,40,512]{2,1,0:T(8,128)(2,1)S(1)} %copy-done, ...), custom_call_target="tpu_custom_call" | custom-call | flops 754974720 | tf_op jit(solution)/shard_map/pallas_call | solution.py:308
  22.6 0.6 %collective-permute-start.8 = (bf16[3,32,512]{2,1,0:T(8,128)(2,1)S(1)}, bf16[3,32,512]{2,1,0:T(8,128)(2,1)S(1)}, u32[]{:S(2)}, u32[]{:S(2)}) collective-permute-start(bf16[3,32,512]{2,1,0:T(8,128)(2,1)S(1)} %get-tuple-element.25.refs_6_), channel_id=1, source_target_pairs={{0,16},{16,0},{1,17},{17,1},{2,18},{18,2},{3,19},{19,3},{4,20},{20... | collective-permute-start | bytes 294920 | tf_op jit(solution)/shard_map/ppermute | solution.py:31
  23.1 1.1 %collective-permute-done.9.refs_2_ = bf16[3,32,512]{2,1,0:T(8,128)(2,1)S(1)} collective-permute-done((bf16[3,32,512]{2,1,0:T(8,128)(2,1)S(1)}, bf16[3,32,512]{2,1,0:T(8,128)(2,1)S(1)}, u32[]{:S(2)}, u32[]{:S(2)}) %collective-permute-start.9) | collective-permute-done | bytes 98336 | tf_op jit(solution)/shard_map/ppermute | solution.py:31
  24.3 0.0 copy-done.1
  24.3 0.0 copy-done.3
  24.3 1.7 %shard_map.78.refs_6_ = f32[640,512]{1,0:T(8,128)S(1)} custom-call(s32[10]{0:T(128)S(1)} %copy-done.3, f32[3,32,512]{2,1,0:T(8,128)S(1)} %get-tuple-element.27.refs_1_, bf16[3,32,512]{2,1,0:T(8,128)(2,1)S(1)} %collective-permute-done.9.refs_2_, bf16[10,40,512]{2,1,0:T(8,128)(2,1)S(1)} %copy-done, f32[10,512]{1,0:T(8,128)S(1)} %copy-done.1, ...), custom_call_target="tpu_custom_call" | custom-call | flops 1006632960 | tf_op jit(solution)/shard_map/pallas_call | solution.py:325
  26.0 1.2 %collective-permute-done.8.refs_2_.refs_1_ = bf16[3,32,512]{2,1,0:T(8,128)(2,1)S(1)} collective-permute-done((bf16[3,32,512]{2,1,0:T(8,128)(2,1)S(1)}, bf16[3,32,512]{2,1,0:T(8,128)(2,1)S(1)}, u32[]{:S(2)}, u32[]{:S(2)}) %collective-permute-start.8) | collective-permute-done | bytes 98336 | tf_op jit(solution)/shard_map/ppermute | solution.py:31
  27.2 1.0 %shard_map.79.refs_3_ = f32[320,512]{1,0:T(8,128)S(1)} custom-call(s32[10]{0:T(128)S(1)} %copy-done.3, f32[2,32,512]{2,1,0:T(8,128)S(1)} %get-tuple-element.26.refs_1_, bf16[3,32,512]{2,1,0:T(8,128)(2,1)S(1)} %collective-permute-done.8.refs_2_.refs_1_, bf16[10,40,512]{2,1,0:T(8,128)(2,1)S(1)} %copy-done, f32[10,512]{1,0:T(8,128)S(1)} %copy-done.1, ...), custom_call_target="tpu_custom_call" | custom-call | flops 335544320 | tf_op jit(solution)/shard_map/pallas_call | solution.py:325
  28.3 0.5 %shard_map.80 = (f32[4,32,640]{2,1,0:T(8,128)S(1)}, bf16[4,32,640]{2,1,0:T(8,128)(2,1)S(1)}) custom-call(f32[32,256]{1,0:T(8,128)S(1)} %get-tuple-element.24.refs_0_, bf16[3,32,512]{2,1,0:T(8,128)(2,1)S(1)} %collective-permute-done.8.refs_2_.refs_1_, bf16[512,20480]{1,0:T(8,128)(2,1)S(1)} %bitcast.5, f32[320,512]{1,0:T(8,128)S(1)} %shard_map.79.refs_3_), custom_call_target="tpu_custom_call" | custom-call | flops 83886080 | tf_op jit(solution)/shard_map/pallas_call | solution.py:344
  28.8 0.1 collective-permute-start.10
  28.9 1.0 %shard_map.81.refs_2_.refs_3_ = f32[320,512]{1,0:T(8,128)S(1)} custom-call(s32[10]{0:T(128)S(1)} %copy-done.3, f32[2,32,512]{2,1,0:T(8,128)S(1)} %get-tuple-element.26.refs_1_, bf16[3,32,512]{2,1,0:T(8,128)(2,1)S(1)} %collective-permute-done.8.refs_2_.refs_1_, bf16[10,40,512]{2,1,0:T(8,128)(2,1)S(1)} %copy-done, f32[10,512]{1,0:T(8,128)S(1)} %copy-done.1, ...), custom_call_target="tpu_custom_call" | custom-call | flops 335544320 | tf_op jit(solution)/shard_map/pallas_call | solution.py:325
  30.0 0.3 collective-permute-done.10.refs_1_
  30.3 0.0 copy-start.4
  30.3 0.5 %shard_map.84 = (f32[4,32,640]{2,1,0:T(8,128)S(1)}, bf16[4,32,640]{2,1,0:T(8,128)(2,1)S(1)}) custom-call(f32[32,256]{1,0:T(8,128)S(1)} %get-tuple-element.24.refs_0_, bf16[3,32,512]{2,1,0:T(8,128)(2,1)S(1)} %collective-permute-done.8.refs_2_.refs_1_, bf16[512,20480]{1,0:T(8,128)(2,1)S(1)} %bitcast.5, f32[320,512]{1,0:T(8,128)S(1)} %shard_map.81.refs_2_.refs_3_, ...), custom_call_target="tpu_custom_call" | custom-call | flops 83886080 | tf_op jit(solution)/shard_map/pallas_call | solution.py:344
  30.9 0.3 collective-permute-start.14
  31.2 0.5 %collective-permute-start.11 = (bf16[2,32,640]{2,1,0:T(8,128)(2,1)S(1)}, bf16[2,32,640]{2,1,0:T(8,128)(2,1)S(1)}, u32[]{:S(2)}, u32[]{:S(2)}) collective-permute-start(bf16[2,32,640]{2,1,0:T(8,128)(2,1)S(1)} %get-tuple-element.32), channel_id=1, source_target_pairs={{0,2},{2,0},{4,6},{6,4},{8,10},{10,8},{12,14},{14,12},{1,3},{3,1},... | collective-permute-start | bytes 245768 | tf_op jit(solution)/shard_map/ppermute | solution.py:31
  31.7 0.7 %collective-permute-done.14.refs_1_ = bf16[4,32,640]{2,1,0:T(8,128)(2,1)S(1)} collective-permute-done((bf16[4,32,640]{2,1,0:T(8,128)(2,1)S(1)}, bf16[4,32,640]{2,1,0:T(8,128)(2,1)S(1)}, u32[]{:S(2)}, u32[]{:S(2)}) %collective-permute-start.14) | collective-permute-done | bytes 163872 | tf_op jit(solution)/shard_map/ppermute | solution.py:31
  32.4 0.9 %collective-permute-start.15 = (bf16[2,32,640]{2,1,0:T(8,128)(2,1)S(1)}, bf16[2,32,640]{2,1,0:T(8,128)(2,1)S(1)}, u32[]{:S(2)}, u32[]{:S(2)}) collective-permute-start(bf16[2,32,640]{2,1,0:T(8,128)(2,1)S(1)} %get-tuple-element.38), channel_id=1, source_target_pairs={{0,2},{2,0},{4,6},{6,4},{8,10},{10,8},{12,14},{14,12},{1,3},{3,1},... | collective-permute-start | bytes 245768 | tf_op jit(solution)/shard_map/ppermute | solution.py:31
  33.3 3.1 %collective-permute-done.11.refs_1_ = bf16[2,32,640]{2,1,0:T(8,128)(2,1)S(1)} collective-permute-done((bf16[2,32,640]{2,1,0:T(8,128)(2,1)S(1)}, bf16[2,32,640]{2,1,0:T(8,128)(2,1)S(1)}, u32[]{:S(2)}, u32[]{:S(2)}) %collective-permute-start.11) | collective-permute-done | bytes 81952 | tf_op jit(solution)/shard_map/ppermute | solution.py:31
  36.4 0.6 %collective-permute-start.12 = (bf16[32,640]{1,0:T(8,128)(2,1)S(1)}, bf16[32,640]{1,0:T(8,128)(2,1)S(1)}, u32[]{:S(2)}, u32[]{:S(2)}) collective-permute-start(bf16[32,640]{1,0:T(8,128)(2,1)S(1)} %get-tuple-element.33), channel_id=1, source_target_pairs={{0,8},{2,10},{4,12},{6,14},{8,0},{10,2},{12,4},{14,6},{1,9},{3,11}... | collective-permute-start | bytes 122888 | tf_op jit(solution)/shard_map/ppermute | solution.py:31
  37.0 1.4 %collective-permute-start.13 = (bf16[32,640]{1,0:T(8,128)(2,1)S(1)}, bf16[32,640]{1,0:T(8,128)(2,1)S(1)}, u32[]{:S(2)}, u32[]{:S(2)}) collective-permute-start(bf16[32,640]{1,0:T(8,128)(2,1)S(1)} %get-tuple-element.34), channel_id=1, source_target_pairs={{0,12},{2,14},{4,8},{6,10},{8,4},{10,6},{12,0},{14,2},{1,13},{3,15... | collective-permute-start | bytes 122888 | tf_op jit(solution)/shard_map/ppermute | solution.py:31
  38.4 0.0 collective-permute-done.15.refs_1_
  38.4 1.6 %collective-permute-start.16 = (bf16[32,640]{1,0:T(8,128)(2,1)S(1)}, bf16[32,640]{1,0:T(8,128)(2,1)S(1)}, u32[]{:S(2)}, u32[]{:S(2)}) collective-permute-start(bf16[32,640]{1,0:T(8,128)(2,1)S(1)} %get-tuple-element.40), channel_id=1, source_target_pairs={{0,4},{2,6},{4,0},{6,2},{8,12},{10,14},{12,8},{14,10},{1,5},{3,7},... | collective-permute-start | bytes 122888 | tf_op jit(solution)/shard_map/ppermute | solution.py:31
  40.0 1.3 %collective-permute-done.12 = bf16[32,640]{1,0:T(8,128)(2,1)S(1)} collective-permute-done((bf16[32,640]{1,0:T(8,128)(2,1)S(1)}, bf16[32,640]{1,0:T(8,128)(2,1)S(1)}, u32[]{:S(2)}, u32[]{:S(2)}) %collective-permute-start.12) | collective-permute-done | bytes 40992 | tf_op jit(solution)/shard_map/ppermute | solution.py:31
  41.3 1.6 %collective-permute-done.13 = bf16[32,640]{1,0:T(8,128)(2,1)S(1)} collective-permute-done((bf16[32,640]{1,0:T(8,128)(2,1)S(1)}, bf16[32,640]{1,0:T(8,128)(2,1)S(1)}, u32[]{:S(2)}, u32[]{:S(2)}) %collective-permute-start.13) | collective-permute-done | bytes 40992 | tf_op jit(solution)/shard_map/ppermute | solution.py:31
  42.9 0.0 collective-permute-done.16
  42.9 0.0 copy-done.4
  42.9 0.7 %fusion = bf16[640,32]{0,1:T(8,128)(2,1)} fusion(bf16[32,640]{1,0:T(8,128)(2,1)S(1)} %collective-permute-done.16, f32[32,640]{1,0:T(8,128)S(1)} %get-tuple-element.39, bf16[32,640]{1,0:T(8,128)(2,1)S(1)} %collective-permute-done.13, bf16[32,640]{1,0:T(8,128)(2,1)S(1)} %collective-permute-done.12, f32[640]{0:T(1024)S(1)} %copy-done.4, ...), kind=kLoop, calls=%fused_computation.1 | loop fusion | flops 204800 | bytes 289280 | tf_op jit(solution)/shard_map/transpose | solution.py:398
  (11 shorter events, 0.1 us)
Async XLA Ops:
  0.0 15.8 %slice-start.5 = ((s8[5242880]{0:T(1024)(128)(4,1)}), s8[4194304]{0:T(1024)(128)(4,1)S(1)}, s32[]{:S(2)}) async-start(s8[5242880]{0:T(1024)(128)(4,1)} %bitcast.6), calls=%async_computation.5 | async-start | bytes 8388608
  0.0 16.0 %slice-start = ((s8[20971520]{0:T(1024)(128)(4,1)}), s8[4194304]{0:T(1024)(128)(4,1)S(1)}, s32[]{:S(2)}) async-start(s8[20971520]{0:T(1024)(128)(4,1)} %bitcast.4), calls=%async_computation | async-start | bytes 8388608
  0.0 15.8 %slice-start.6 = ((s8[5242880]{0:T(1024)(128)(4,1)}), s8[1048576]{0:T(1024)(128)(4,1)S(1)}, s32[]{:S(2)}) async-start(s8[5242880]{0:T(1024)(128)(4,1)} %bitcast.6), calls=%async_computation.6 | async-start | bytes 2097152
  0.0 15.8 %copy-start.2 = (bf16[640,32]{0,1:T(8,128)(2,1)S(1)}, bf16[640,32]{0,1:T(8,128)(2,1)}, u32[]{:S(2)}) copy-start(bf16[640,32]{0,1:T(8,128)(2,1)} %param.7) | copy-start | bytes 122884
  0.0 16.0 %slice-start.1 = ((s8[20971520]{0:T(1024)(128)(4,1)}), s8[4194304]{0:T(1024)(128)(4,1)S(1)}, s32[]{:S(2)}) async-start(s8[20971520]{0:T(1024)(128)(4,1)} %bitcast.4), calls=%async_computation.1 | async-start | bytes 8388608
  0.0 16.0 %slice-start.2 = ((s8[20971520]{0:T(1024)(128)(4,1)}), s8[4194304]{0:T(1024)(128)(4,1)S(1)}, s32[]{:S(2)}) async-start(s8[20971520]{0:T(1024)(128)(4,1)} %bitcast.4), calls=%async_computation.2 | async-start | bytes 8388608
  0.0 16.0 %slice-start.3 = ((s8[20971520]{0:T(1024)(128)(4,1)}), s8[4194304]{0:T(1024)(128)(4,1)S(1)}, s32[]{:S(2)}) async-start(s8[20971520]{0:T(1024)(128)(4,1)} %bitcast.4), calls=%async_computation.3 | async-start | bytes 8388608
  0.0 16.0 %slice-start.4 = ((s8[20971520]{0:T(1024)(128)(4,1)}), s8[4194304]{0:T(1024)(128)(4,1)S(1)}, s32[]{:S(2)}) async-start(s8[20971520]{0:T(1024)(128)(4,1)} %bitcast.4), calls=%async_computation.4 | async-start | bytes 8388608
  0.0 7.5 %collective-permute-start.5 = (bf16[32,640]{1,0:T(8,128)(2,1)}, bf16[32,640]{1,0:T(8,128)(2,1)S(1)}, u32[]{:S(2)}, u32[]{:S(2)}) collective-permute-start(bf16[32,640]{1,0:T(8,128)(2,1)} %bitcast.8), channel_id=1, source_target_pairs={{0,12},{2,14},{4,8},{6,10},{8,4},{10,6},{12,0},{14,2},{1,13},{3,15... | collective-permute-start | bytes 122888 | tf_op jit(solution)/shard_map/ppermute | solution.py:31
  5.2 5.1 %collective-permute-start.3 = (bf16[32,640]{1,0:T(8,128)(2,1)}, bf16[32,640]{1,0:T(8,128)(2,1)S(1)}, u32[]{:S(2)}, u32[]{:S(2)}) collective-permute-start(bf16[32,640]{1,0:T(8,128)(2,1)} %bitcast.9), channel_id=1, source_target_pairs={{0,8},{2,10},{4,12},{6,14},{8,0},{10,2},{12,4},{14,6},{1,9},{3,11}... | collective-permute-start | bytes 122888 | tf_op jit(solution)/shard_map/ppermute | solution.py:31
  5.2 6.6 %collective-permute-start.1 = (bf16[32,640]{1,0:T(8,128)(2,1)}, bf16[32,640]{1,0:T(8,128)(2,1)S(1)}, u32[]{:S(2)}, u32[]{:S(2)}) collective-permute-start(bf16[32,640]{1,0:T(8,128)(2,1)} %bitcast.10), channel_id=1, source_target_pairs={{0,4},{2,6},{4,0},{6,2},{8,12},{10,14},{12,8},{14,10},{1,5},{3,7},... | collective-permute-start | bytes 122888 | tf_op jit(solution)/shard_map/ppermute | solution.py:31
  5.8 6.5 %collective-permute-start = (bf16[32,640]{1,0:T(8,128)(2,1)}, bf16[32,640]{1,0:T(8,128)(2,1)S(1)}, u32[]{:S(2)}, u32[]{:S(2)}) collective-permute-start(bf16[32,640]{1,0:T(8,128)(2,1)} %bitcast.11), channel_id=1, source_target_pairs={{0,2},{2,0},{4,6},{6,4},{8,10},{10,8},{12,14},{14,12},{1,3},{3,1},... | collective-permute-start | bytes 122888 | tf_op jit(solution)/shard_map/ppermute | solution.py:31
  7.5 4.8 %collective-permute-start.6 = (bf16[32,640]{1,0:T(8,128)(2,1)S(1)}, bf16[32,640]{1,0:T(8,128)(2,1)S(1)}, u32[]{:S(2)}, u32[]{:S(2)}) collective-permute-start(bf16[32,640]{1,0:T(8,128)(2,1)S(1)} %shard_map.73.refs_7_), channel_id=1, source_target_pairs={{0,2},{2,0},{4,6},{6,4},{8,10},{10,8},{12,14},{14,12},{1,3},{3,1},... | collective-permute-start | bytes 122888 | tf_op jit(solution)/shard_map/ppermute | solution.py:31
  10.3 4.0 %collective-permute-start.4 = (bf16[32,640]{1,0:T(8,128)(2,1)S(1)}, bf16[32,640]{1,0:T(8,128)(2,1)S(1)}, u32[]{:S(2)}, u32[]{:S(2)}) collective-permute-start(bf16[32,640]{1,0:T(8,128)(2,1)S(1)} %collective-permute-done.3.refs_5_), channel_id=1, source_target_pairs={{0,2},{2,0},{4,6},{6,4},{8,10},{10,8},{12,14},{14,12},{1,3},{3,1},... | collective-permute-start | bytes 122888 | tf_op jit(solution)/shard_map/ppermute | solution.py:31
  11.8 4.0 %collective-permute-start.2 = (bf16[32,640]{1,0:T(8,128)(2,1)S(1)}, bf16[32,640]{1,0:T(8,128)(2,1)S(1)}, u32[]{:S(2)}, u32[]{:S(2)}) collective-permute-start(bf16[32,640]{1,0:T(8,128)(2,1)S(1)} %collective-permute-done.1.refs_3_), channel_id=1, source_target_pairs={{0,2},{2,0},{4,6},{6,4},{8,10},{10,8},{12,14},{14,12},{1,3},{3,1},... | collective-permute-start | bytes 122888 | tf_op jit(solution)/shard_map/ppermute | solution.py:31
  15.9 1.7 %copy-start = (bf16[10,40,512]{2,1,0:T(8,128)(2,1)S(1)}, bf16[10,40,512]{2,1,0:T(8,128)(2,1)}, u32[]{:S(2)}) copy-start(bf16[10,40,512]{2,1,0:T(8,128)(2,1)} %refs_3_.7) | copy-start | bytes 1228804
  15.9 1.7 %collective-permute-start.7 = (bf16[8,32,640]{2,1,0:T(8,128)(2,1)S(1)}, bf16[8,32,640]{2,1,0:T(8,128)(2,1)S(1)}, u32[]{:S(2)}, u32[]{:S(2)}) collective-permute-start(bf16[8,32,640]{2,1,0:T(8,128)(2,1)S(1)} %shard_map.74.refs_0_), channel_id=1, source_target_pairs={{0,1},{1,0},{2,3},{3,2},{4,5},{5,4},{6,7},{7,6},{8,9},{9,8},{10,11... | collective-permute-start | bytes 983048 | tf_op jit(solution)/shard_map/ppermute | solution.py:31
  19.4 4.9 %collective-permute-start.9 = (bf16[3,32,512]{2,1,0:T(8,128)(2,1)S(1)}, bf16[3,32,512]{2,1,0:T(8,128)(2,1)S(1)}, u32[]{:S(2)}, u32[]{:S(2)}) collective-permute-start(bf16[3,32,512]{2,1,0:T(8,128)(2,1)S(1)} %get-tuple-element.28), channel_id=1, source_target_pairs={{0,16},{16,0},{1,17},{17,1},{2,18},{18,2},{3,19},{19,3},{4,20},{20... | collective-permute-start | bytes 294920 | tf_op jit(solution)/shard_map/ppermute | solution.py:31
  21.0 3.3 %copy-start.1 = (f32[10,512]{1,0:T(8,128)S(1)}, f32[10,512]{1,0:T(8,128)}, u32[]{:S(2)}) copy-start(f32[10,512]{1,0:T(8,128)} %refs_4_.7) | copy-start | bytes 61444
  21.0 3.3 %copy-start.3 = (s32[10]{0:T(128)S(1)}, s32[10]{0:T(128)}, u32[]{:S(2)}) copy-start(s32[10]{0:T(128)} %refs_0_.7) | copy-start | bytes 124
  22.6 4.7 %collective-permute-start.8 = (bf16[3,32,512]{2,1,0:T(8,128)(2,1)S(1)}, bf16[3,32,512]{2,1,0:T(8,128)(2,1)S(1)}, u32[]{:S(2)}, u32[]{:S(2)}) collective-permute-start(bf16[3,32,512]{2,1,0:T(8,128)(2,1)S(1)} %get-tuple-element.25.refs_6_), channel_id=1, source_target_pairs={{0,16},{16,0},{1,17},{17,1},{2,18},{18,2},{3,19},{19,3},{4,20},{20... | collective-permute-start | bytes 294920 | tf_op jit(solution)/shard_map/ppermute | solution.py:31
  28.8 1.5 %collective-permute-start.10 = (bf16[4,32,640]{2,1,0:T(8,128)(2,1)S(1)}, bf16[4,32,640]{2,1,0:T(8,128)(2,1)S(1)}, u32[]{:S(2)}, u32[]{:S(2)}) collective-permute-start(bf16[4,32,640]{2,1,0:T(8,128)(2,1)S(1)} %get-tuple-element.30), channel_id=1, source_target_pairs={{0,1},{1,0},{2,3},{3,2},{4,5},{5,4},{6,7},{7,6},{8,9},{9,8},{10,11... | collective-permute-start | bytes 491528 | tf_op jit(solution)/shard_map/ppermute | solution.py:31
  30.3 12.6 %copy-start.4 = (f32[640]{0:T(1024)S(1)}, f32[640]{0:T(1024)}, u32[]{:S(2)}) copy-start(f32[640]{0:T(1024)} %param.8) | copy-start | bytes 7684
  30.9 1.5 %collective-permute-start.14 = (bf16[4,32,640]{2,1,0:T(8,128)(2,1)S(1)}, bf16[4,32,640]{2,1,0:T(8,128)(2,1)S(1)}, u32[]{:S(2)}, u32[]{:S(2)}) collective-permute-start(bf16[4,32,640]{2,1,0:T(8,128)(2,1)S(1)} %get-tuple-element.36), channel_id=1, source_target_pairs={{0,1},{1,0},{2,3},{3,2},{4,5},{5,4},{6,7},{7,6},{8,9},{9,8},{10,11... | collective-permute-start | bytes 491528 | tf_op jit(solution)/shard_map/ppermute | solution.py:31
  31.2 5.2 %collective-permute-start.11 = (bf16[2,32,640]{2,1,0:T(8,128)(2,1)S(1)}, bf16[2,32,640]{2,1,0:T(8,128)(2,1)S(1)}, u32[]{:S(2)}, u32[]{:S(2)}) collective-permute-start(bf16[2,32,640]{2,1,0:T(8,128)(2,1)S(1)} %get-tuple-element.32), channel_id=1, source_target_pairs={{0,2},{2,0},{4,6},{6,4},{8,10},{10,8},{12,14},{14,12},{1,3},{3,1},... | collective-permute-start | bytes 245768 | tf_op jit(solution)/shard_map/ppermute | solution.py:31
  32.4 6.0 %collective-permute-start.15 = (bf16[2,32,640]{2,1,0:T(8,128)(2,1)S(1)}, bf16[2,32,640]{2,1,0:T(8,128)(2,1)S(1)}, u32[]{:S(2)}, u32[]{:S(2)}) collective-permute-start(bf16[2,32,640]{2,1,0:T(8,128)(2,1)S(1)} %get-tuple-element.38), channel_id=1, source_target_pairs={{0,2},{2,0},{4,6},{6,4},{8,10},{10,8},{12,14},{14,12},{1,3},{3,1},... | collective-permute-start | bytes 245768 | tf_op jit(solution)/shard_map/ppermute | solution.py:31
  36.4 5.0 %collective-permute-start.12 = (bf16[32,640]{1,0:T(8,128)(2,1)S(1)}, bf16[32,640]{1,0:T(8,128)(2,1)S(1)}, u32[]{:S(2)}, u32[]{:S(2)}) collective-permute-start(bf16[32,640]{1,0:T(8,128)(2,1)S(1)} %get-tuple-element.33), channel_id=1, source_target_pairs={{0,8},{2,10},{4,12},{6,14},{8,0},{10,2},{12,4},{14,6},{1,9},{3,11}... | collective-permute-start | bytes 122888 | tf_op jit(solution)/shard_map/ppermute | solution.py:31
  37.0 5.9 %collective-permute-start.13 = (bf16[32,640]{1,0:T(8,128)(2,1)S(1)}, bf16[32,640]{1,0:T(8,128)(2,1)S(1)}, u32[]{:S(2)}, u32[]{:S(2)}) collective-permute-start(bf16[32,640]{1,0:T(8,128)(2,1)S(1)} %get-tuple-element.34), channel_id=1, source_target_pairs={{0,12},{2,14},{4,8},{6,10},{8,4},{10,6},{12,0},{14,2},{1,13},{3,15... | collective-permute-start | bytes 122888 | tf_op jit(solution)/shard_map/ppermute | solution.py:31
  38.4 4.5 %collective-permute-start.16 = (bf16[32,640]{1,0:T(8,128)(2,1)S(1)}, bf16[32,640]{1,0:T(8,128)(2,1)S(1)}, u32[]{:S(2)}, u32[]{:S(2)}) collective-permute-start(bf16[32,640]{1,0:T(8,128)(2,1)S(1)} %get-tuple-element.40), channel_id=1, source_target_pairs={{0,4},{2,6},{4,0},{6,2},{8,12},{10,14},{12,8},{14,10},{1,5},{3,7},... | collective-permute-start | bytes 122888 | tf_op jit(solution)/shard_map/ppermute | solution.py:31
where the time goes:
time: 43.7 us; the launch traced here: 43.6 us
  starting transfers between devices  18.9 us (43%)
  waiting for transfers between devices  14.5 us (33%)
  Pallas kernels  9.26 us (21%)
  other arithmetic  0.65 us (1%)
    ppermute x17, starting transfers between devices, swap(): return lax.ppermute(x, axis, [(i, i ^ mask) for i in range(count)])  18.9 us
    ppermute x17, waiting for transfers between devices, swap(): return lax.ppermute(x, axis, [(i, i ^ mask) for i in range(count)])  14.5 us
    pallas_call x3, Pallas kernels, grid(): call(after(body, count) if len(more) + 6 > count else body, shape((used *...  3.82 us
    pallas_call x1, Pallas kernels, local(): call(after(bind(first_dens_kernel, spans[0]), 4), (shape(chunks[0], f32),...  1.78 us
    pallas_call x1, Pallas kernels, local(): call(bind(second_dens_kernel, spans[1]), (shape(chunks[1], f32), shape((l...  1.59 us
    pallas_call x2, Pallas kernels, back(): call(after(body, 4) if order else body, (shape(share, f32), shape(share,...  1.07 us
  transfers between devices with their start and end apart: 17, of which 11 were waited for; matrix products, arithmetic and copies ran while one was open for 0% of the time, Pallas kernels for 12%

commit v1 on v0

--- a/solution.py
+++ b/solution.py
@@ -69,7 +69,7 @@
         stride, radix = self.digits[-1]
         self.top = stride
         if self.aligned and radix == 4 and len(self.digits) == 2 and self.occs % radix == 0:
-            self.parts = [(2, 3), (0, 1)]
+            self.parts = [(3, 2), (0, 1)]
             self.run = self.occs // radix
         else:
             assert not self.aligned
@@ -115,6 +115,15 @@
 def stack_kernel(plan, *refs):
     for m, piece in enumerate(refs[:-1]):
         refs[-1][m] = piece[...]
+
+
+def place_kernel(plan, slots, *refs):
+    for slot, piece in zip(slots, refs):
+        if isinstance(slot, tuple):
+            for n, m in enumerate(slot):
+                refs[-1][m] = piece[n]
+        else:
+            refs[-1][slot] = piece[...]
 
 
 def occ_rows(plan, occ, b, occ32):
@@ -261,6 +270,15 @@
     pieces, masks = [trial_cols], [0]
     for stride, radix in reversed(digits):
         known = len(masks)
+        if len(plan.parts) == 2 and known > 2:
+            pair = call(
+                bind(stack_kernel), shape((2,) + trial_cols.shape, bf16), [VMEM] * 2
+            )(pieces[1], pieces[2])
+            for n in (0, known - 1):
+                pieces.append(swap(pieces[n], "blk", blks, stride))
+            pieces.append(swap(pair, "blk", blks, stride))
+            masks += [masks[n] ^ stride for n in (0, known - 1)]
+            break
         for d in range(1, radix):
             for n in range(known):
                 pieces.append(swap(pieces[n], "blk", blks, d * stride))
@@ -269,11 +287,14 @@
             pieces[-1] = call(
                 bind(copy_kernel), shape(trial_cols.shape, bf16), [VMEM], flops=HEAD
             )(pieces[-1])
-    pieces = [p for _, p in sorted(zip(masks, pieces), key=lambda pair: pair[0])]
+    if len(plan.parts) == 2:
+        slots = tuple(masks) + (tuple(masks[n] ^ stride for n in (1, 2)),)
+    else:
+        pieces = [p for _, p in sorted(zip(masks, pieces), key=lambda pair: pair[0])]
 
     if plan.aligned:
         mine = call(
-            after(bind(stack_kernel), 0), shape(half, bf16), [VMEM] * (len(pieces) + 1)
+            after(bind(place_kernel, slots), 0), shape(half, bf16), [VMEM] * (len(pieces) + 1)
         )(vir_values, *pieces)
         other = swap(mine, "vec", vecs, 1)
     else:

time: 43.7 us -> 45 us (1.030)
  starting transfers between devices: 18.9 us -> 20.3 us
  waiting for transfers between devices: 14.5 us -> 13.3 us
  local copies, waits for them, and re-layouts: 0.05 us -> 1.05 us
    ppermute x17 -> x16, starting transfers between devices: 18.9 us -> 20.3 us  [swap(): return lax.ppermute(x, axis, [(i, i ^ mask) for i in range(count)])]
    ppermute x17 -> x16, waiting for transfers between devices: 14.5 us -> 13.3 us  [swap(): return lax.ppermute(x, axis, [(i, i ^ mask) for i in range(count)])]
    unnamed x24, local copies, waits for them, and re-layouts: 0.05 us -> 1.05 us
  transfers between devices with their start and end apart: 17 -> 16, of which waited for: 11 -> 9; matrix products, arithmetic and copies ran while one was open for 0% -> 0% of each run, Pallas kernels for 12% -> 12%
where the time goes in v1:
time: 45 us; the launch traced here: 44.9 us
  starting transfers between devices  20.3 us (45%)
  waiting for transfers between devices  13.3 us (30%)
  Pallas kernels  9.27 us (21%)
  local copies, waits for them, and re-layouts  1.05 us (2%)
  other arithmetic  0.65 us (1%)
    ppermute x16, starting transfers between devices, swap(): return lax.ppermute(x, axis, [(i, i ^ mask) for i in range(count)])  20.3 us
    ppermute x16, waiting for transfers between devices, swap(): return lax.ppermute(x, axis, [(i, i ^ mask) for i in range(count)])  13.3 us
    pallas_call x3, Pallas kernels, grid(): call(after(body, count) if len(more) + 6 > count else body, shape((used *...  3.82 us
    pallas_call x1, Pallas kernels, local(): call(after(bind(first_dens_kernel, spans[0]), 4), (shape(chunks[0], f32),...  1.79 us
    pallas_call x1, Pallas kernels, local(): call(bind(second_dens_kernel, spans[1]), (shape(chunks[1], f32), shape((l...  1.59 us
    pallas_call x2, Pallas kernels, back(): call(after(body, 4) if order else body, (shape(share, f32), shape(share,...  1.07 us
    unnamed x24, local copies, waits for them, and re-layouts  1.05 us
  transfers between devices with their start and end apart: 16, of which 9 were waited for; matrix products, arithmetic and copies ran while one was open for 0% of the time, Pallas kernels for 12%

profile of v1, /device:TPU:0, one launch (start us, length us, event | category | flops | bytes accessed | tf_op | source)
XLA Modules:
  0.0 44.9 jit_solution(813860054372873117)
XLA Ops:
  0.0 4.1 %collective-permute-start.1 = (bf16[32,640]{1,0:T(8,128)(2,1)}, bf16[32,640]{1,0:T(8,128)(2,1)S(1)}, u32[]{:S(2)}, u32[]{:S(2)}) collective-permute-start(bf16[32,640]{1,0:T(8,128)(2,1)} %bitcast.8), channel_id=1, source_target_pairs={{0,8},{2,10},{4,12},{6,14},{8,0},{10,2},{12,4},{14,6},{1,9},{3,11}... | collective-permute-start | bytes 122888 | tf_op jit(solution)/shard_map/ppermute | solution.py:31
  4.1 1.6 %collective-permute-start = (bf16[32,640]{1,0:T(8,128)(2,1)}, bf16[32,640]{1,0:T(8,128)(2,1)S(1)}, u32[]{:S(2)}, u32[]{:S(2)}) collective-permute-start(bf16[32,640]{1,0:T(8,128)(2,1)} %bitcast.9), channel_id=1, source_target_pairs={{0,4},{2,6},{4,0},{6,2},{8,12},{10,14},{12,8},{14,10},{1,5},{3,7},... | collective-permute-start | bytes 122888 | tf_op jit(solution)/shard_map/ppermute | solution.py:31
  5.6 0.0 collective-permute-start.2
  5.6 1.7 %collective-permute-start.3 = (bf16[32,640]{1,0:T(8,128)(2,1)}, bf16[32,640]{1,0:T(8,128)(2,1)S(1)}, u32[]{:S(2)}, u32[]{:S(2)}) collective-permute-start(bf16[32,640]{1,0:T(8,128)(2,1)} %bitcast.11), channel_id=1, source_target_pairs={{0,2},{2,0},{4,6},{6,4},{8,10},{10,8},{12,14},{14,12},{1,3},{3,1},... | collective-permute-start | bytes 122888 | tf_op jit(solution)/shard_map/ppermute | solution.py:31
  7.4 0.0 collective-permute-done.1.refs_1_.refs_3_
  7.4 0.9 %collective-permute-done.refs_0_.refs_2_ = bf16[32,640]{1,0:T(8,128)(2,1)S(1)} collective-permute-done((bf16[32,640]{1,0:T(8,128)(2,1)}, bf16[32,640]{1,0:T(8,128)(2,1)S(1)}, u32[]{:S(2)}, u32[]{:S(2)}) %collective-permute-start) | collective-permute-done | bytes 40992 | tf_op jit(solution)/shard_map/ppermute | solution.py:31
  8.3 0.0 slice-start
  8.3 0.0 slice-start.6
  8.3 0.0 copy-start.2
  8.3 0.0 slice-start.1
  8.3 0.0 slice-start.2
  8.3 0.0 slice-start.3
  8.4 0.0 slice-start.4
  8.4 1.6 %collective-permute-start.5 = (bf16[2,32,640]{2,1,0:T(8,128)(2,1)S(1)}, bf16[2,32,640]{2,1,0:T(8,128)(2,1)S(1)}, u32[]{:S(2)}, u32[]{:S(2)}) collective-permute-start(bf16[2,32,640]{2,1,0:T(8,128)(2,1)S(1)} %shard_map.74), channel_id=1, source_target_pairs={{0,2},{2,0},{4,6},{6,4},{8,10},{10,8},{12,14},{14,12},{1,3},{3,1},... | collective-permute-start | bytes 245768 | tf_op jit(solution)/shard_map/ppermute | solution.py:31
  10.0 1.7 %collective-permute-done.2.refs_0_ = bf16[32,640]{1,0:T(8,128)(2,1)S(1)} collective-permute-done((bf16[32,640]{1,0:T(8,128)(2,1)}, bf16[32,640]{1,0:T(8,128)(2,1)S(1)}, u32[]{:S(2)}, u32[]{:S(2)}) %collective-permute-start.2) | collective-permute-done | bytes 40992 | tf_op jit(solution)/shard_map/ppermute | solution.py:31
  11.7 1.5 %collective-permute-start.4 = (bf16[32,640]{1,0:T(8,128)(2,1)S(1)}, bf16[32,640]{1,0:T(8,128)(2,1)S(1)}, u32[]{:S(2)}, u32[]{:S(2)}) collective-permute-start(bf16[32,640]{1,0:T(8,128)(2,1)S(1)} %shard_map.73.refs_4_), channel_id=1, source_target_pairs={{0,2},{2,0},{4,6},{6,4},{8,10},{10,8},{12,14},{14,12},{1,3},{3,1},... | collective-permute-start | bytes 122888 | tf_op jit(solution)/shard_map/ppermute | solution.py:31
  13.2 0.0 collective-permute-done.3.refs_5_
  13.2 2.5 %collective-permute-done.4.refs_6_ = bf16[32,640]{1,0:T(8,128)(2,1)S(1)} collective-permute-done((bf16[32,640]{1,0:T(8,128)(2,1)S(1)}, bf16[32,640]{1,0:T(8,128)(2,1)S(1)}, u32[]{:S(2)}, u32[]{:S(2)}) %collective-permute-start.4) | collective-permute-done | bytes 40992 | tf_op jit(solution)/shard_map/ppermute | solution.py:31
  15.7 0.0 collective-permute-done.5.refs_7_
  15.7 0.0 slice-done.5
  15.7 0.0 slice-done.6
  15.7 0.0 copy-done.2
  15.7 0.0 copy-start
  15.7 0.1 collective-permute-start.6
  15.8 0.0 slice-done
  15.8 0.0 slice-done.1
  15.8 0.0 slice-done.2
  15.8 0.0 slice-done.3
  15.9 1.0 %slice-done.4 = s8[4194304]{0:T(1024)(128)(4,1)S(1)} async-done(((s8[20971520]{0:T(1024)(128)(4,1)}), s8[4194304]{0:T(1024)(128)(4,1)S(1)}, s32[]{:S(2)}) %slice-start.4) | async-done | bytes 4194328
  16.9 0.8 %shard_map.76.refs_4_.refs_5_ = f32[32,256]{1,0:T(8,128)S(1)} custom-call(bf16[8,32,640]{2,1,0:T(8,128)(2,1)S(1)} %shard_map.75.refs_0_, bf16[512,20480]{1,0:T(8,128)(2,1)S(1)} %bitcast.5), custom_call_target="tpu_custom_call" | custom-call | flops 83886080 | tf_op jit(solution)/shard_map/pallas_call | solution.py:309
  17.7 0.0 collective-permute-done.6.refs_1_.refs_3_
  17.7 0.0 copy-done
  17.7 1.8 %shard_map.77 = (f32[3,32,512]{2,1,0:T(8,128)S(1)}, bf16[3,32,512]{2,1,0:T(8,128)(2,1)S(1)}, bf16[640,512]{1,0:T(8,128)(2,1)S(1)}) custom-call(bf16[8,32,640]{2,1,0:T(8,128)(2,1)S(1)} %shard_map.75.refs_0_, bf16[8,32,640]{2,1,0:T(8,128)(2,1)S(1)} %collective-permute-done.6.refs_1_.refs_3_, bf16[10,512,512]{2,1,0:T(8,128)(2,1)S(1)} %bitcast.7, ...), custom_call_target="tpu_custom_call" | custom-call | flops 1006632960 | tf_op jit(solution)/shard_map/pallas_call | solution.py:321
  19.5 1.6 %collective-permute-start.8 = (bf16[3,32,512]{2,1,0:T(8,128)(2,1)S(1)}, bf16[3,32,512]{2,1,0:T(8,128)(2,1)S(1)}, u32[]{:S(2)}, u32[]{:S(2)}) collective-permute-start(bf16[3,32,512]{2,1,0:T(8,128)(2,1)S(1)} %get-tuple-element.28), channel_id=1, source_target_pairs={{0,16},{16,0},{1,17},{17,1},{2,18},{18,2},{3,19},{19,3},{4,20},{20... | collective-permute-start | bytes 294920 | tf_op jit(solution)/shard_map/ppermute | solution.py:31
  21.1 0.0 copy-start.1
  21.1 0.0 copy-start.3
  21.1 1.6 %shard_map.78 = (f32[2,32,512]{2,1,0:T(8,128)S(1)}, bf16[3,32,512]{2,1,0:T(8,128)(2,1)S(1)}, f32[32,256]{1,0:T(8,128)S(1)}) custom-call(bf16[640,512]{1,0:T(8,128)(2,1)S(1)} %get-tuple-element.23.refs_0_, bf16[10,512,512]{2,1,0:T(8,128)(2,1)S(1)} %bitcast.7, bf16[10,40,512]{2,1,0:T(8,128)(2,1)S(1)} %copy-done, ...), custom_call_target="tpu_custom_call" | custom-call | flops 754974720 | tf_op jit(solution)/shard_map/pallas_call | solution.py:329
  22.7 0.6 %collective-permute-start.7 = (bf16[3,32,512]{2,1,0:T(8,128)(2,1)S(1)}, bf16[3,32,512]{2,1,0:T(8,128)(2,1)S(1)}, u32[]{:S(2)}, u32[]{:S(2)}) collective-permute-start(bf16[3,32,512]{2,1,0:T(8,128)(2,1)S(1)} %get-tuple-element.25.refs_6_), channel_id=1, source_target_pairs={{0,16},{16,0},{1,17},{17,1},{2,18},{18,2},{3,19},{19,3},{4,20},{20... | collective-permute-start | bytes 294920 | tf_op jit(solution)/shard_map/ppermute | solution.py:31
  23.3 0.9 %collective-permute-done.8.refs_2_ = bf16[3,32,512]{2,1,0:T(8,128)(2,1)S(1)} collective-permute-done((bf16[3,32,512]{2,1,0:T(8,128)(2,1)S(1)}, bf16[3,32,512]{2,1,0:T(8,128)(2,1)S(1)}, u32[]{:S(2)}, u32[]{:S(2)}) %collective-permute-start.8) | collective-permute-done | bytes 98336 | tf_op jit(solution)/shard_map/ppermute | solution.py:31
  24.2 0.0 copy-done.1
  24.2 0.0 copy-done.3
  24.2 1.7 %shard_map.79.refs_6_ = f32[640,512]{1,0:T(8,128)S(1)} custom-call(s32[10]{0:T(128)S(1)} %copy-done.3, f32[3,32,512]{2,1,0:T(8,128)S(1)} %get-tuple-element.27.refs_1_, bf16[3,32,512]{2,1,0:T(8,128)(2,1)S(1)} %collective-permute-done.8.refs_2_, bf16[10,40,512]{2,1,0:T(8,128)(2,1)S(1)} %copy-done, f32[10,512]{1,0:T(8,128)S(1)} %copy-done.1, ...), custom_call_target="tpu_custom_call" | custom-call | flops 1006632960 | tf_op jit(solution)/shard_map/pallas_call | solution.py:346
  25.9 1.4 %collective-permute-done.7.refs_2_.refs_1_ = bf16[3,32,512]{2,1,0:T(8,128)(2,1)S(1)} collective-permute-done((bf16[3,32,512]{2,1,0:T(8,128)(2,1)S(1)}, bf16[3,32,512]{2,1,0:T(8,128)(2,1)S(1)}, u32[]{:S(2)}, u32[]{:S(2)}) %collective-permute-start.7) | collective-permute-done | bytes 98336 | tf_op jit(solution)/shard_map/ppermute | solution.py:31
  27.4 1.1 %shard_map.80.refs_3_ = f32[320,512]{1,0:T(8,128)S(1)} custom-call(s32[10]{0:T(128)S(1)} %copy-done.3, f32[2,32,512]{2,1,0:T(8,128)S(1)} %get-tuple-element.26.refs_1_, bf16[3,32,512]{2,1,0:T(8,128)(2,1)S(1)} %collective-permute-done.7.refs_2_.refs_1_, bf16[10,40,512]{2,1,0:T(8,128)(2,1)S(1)} %copy-done, f32[10,512]{1,0:T(8,128)S(1)} %copy-done.1, ...), custom_call_target="tpu_custom_call" | custom-call | flops 335544320 | tf_op jit(solution)/shard_map/pallas_call | solution.py:346
  28.4 0.5 %shard_map.81 = (f32[4,32,640]{2,1,0:T(8,128)S(1)}, bf16[4,32,640]{2,1,0:T(8,128)(2,1)S(1)}) custom-call(f32[32,256]{1,0:T(8,128)S(1)} %get-tuple-element.24.refs_0_, bf16[3,32,512]{2,1,0:T(8,128)(2,1)S(1)} %collective-permute-done.7.refs_2_.refs_1_, bf16[512,20480]{1,0:T(8,128)(2,1)S(1)} %bitcast.5, f32[320,512]{1,0:T(8,128)S(1)} %shard_map.80.refs_3_), custom_call_target="tpu_custom_call" | custom-call | flops 83886080 | tf_op jit(solution)/shard_map/pallas_call | solution.py:365
  29.0 0.1 collective-permute-start.9
  29.0 1.0 %shard_map.82.refs_2_.refs_3_ = f32[320,512]{1,0:T(8,128)S(1)} custom-call(s32[10]{0:T(128)S(1)} %copy-done.3, f32[2,32,512]{2,1,0:T(8,128)S(1)} %get-tuple-element.26.refs_1_, bf16[3,32,512]{2,1,0:T(8,128)(2,1)S(1)} %collective-permute-done.7.refs_2_.refs_1_, bf16[10,40,512]{2,1,0:T(8,128)(2,1)S(1)} %copy-done, f32[10,512]{1,0:T(8,128)S(1)} %copy-done.1, ...), custom_call_target="tpu_custom_call" | custom-call | flops 335544320 | tf_op jit(solution)/shard_map/pallas_call | solution.py:346
  30.1 0.3 collective-permute-done.9.refs_1_
  30.5 0.0 copy-start.4
  30.5 0.5 %shard_map.85 = (f32[4,32,640]{2,1,0:T(8,128)S(1)}, bf16[4,32,640]{2,1,0:T(8,128)(2,1)S(1)}) custom-call(f32[32,256]{1,0:T(8,128)S(1)} %get-tuple-element.24.refs_0_, bf16[3,32,512]{2,1,0:T(8,128)(2,1)S(1)} %collective-permute-done.7.refs_2_.refs_1_, bf16[512,20480]{1,0:T(8,128)(2,1)S(1)} %bitcast.5, f32[320,512]{1,0:T(8,128)S(1)} %shard_map.82.refs_2_.refs_3_, ...), custom_call_target="tpu_custom_call" | custom-call | flops 83886080 | tf_op jit(solution)/shard_map/pallas_call | solution.py:365
  31.0 0.3 collective-permute-start.13
  31.3 1.5 %collective-permute-start.10 = (bf16[2,32,640]{2,1,0:T(8,128)(2,1)S(1)}, bf16[2,32,640]{2,1,0:T(8,128)(2,1)S(1)}, u32[]{:S(2)}, u32[]{:S(2)}) collective-permute-start(bf16[2,32,640]{2,1,0:T(8,128)(2,1)S(1)} %get-tuple-element.32), channel_id=1, source_target_pairs={{0,2},{2,0},{4,6},{6,4},{8,10},{10,8},{12,14},{14,12},{1,3},{3,1},... | collective-permute-start | bytes 245768 | tf_op jit(solution)/shard_map/ppermute | solution.py:31
  32.8 0.0 collective-permute-done.13.refs_1_
  32.8 1.2 %collective-permute-start.14 = (bf16[2,32,640]{2,1,0:T(8,128)(2,1)S(1)}, bf16[2,32,640]{2,1,0:T(8,128)(2,1)S(1)}, u32[]{:S(2)}, u32[]{:S(2)}) collective-permute-start(bf16[2,32,640]{2,1,0:T(8,128)(2,1)S(1)} %get-tuple-element.38), channel_id=1, source_target_pairs={{0,2},{2,0},{4,6},{6,4},{8,10},{10,8},{12,14},{14,12},{1,3},{3,1},... | collective-permute-start | bytes 245768 | tf_op jit(solution)/shard_map/ppermute | solution.py:31
  34.1 2.3 %collective-permute-done.10.refs_1_ = bf16[2,32,640]{2,1,0:T(8,128)(2,1)S(1)} collective-permute-done((bf16[2,32,640]{2,1,0:T(8,128)(2,1)S(1)}, bf16[2,32,640]{2,1,0:T(8,128)(2,1)S(1)}, u32[]{:S(2)}, u32[]{:S(2)}) %collective-permute-start.10) | collective-permute-done | bytes 81952 | tf_op jit(solution)/shard_map/ppermute | solution.py:31
  36.4 2.9 %collective-permute-start.11 = (bf16[32,640]{1,0:T(8,128)(2,1)S(1)}, bf16[32,640]{1,0:T(8,128)(2,1)S(1)}, u32[]{:S(2)}, u32[]{:S(2)}) collective-permute-start(bf16[32,640]{1,0:T(8,128)(2,1)S(1)} %get-tuple-element.33), channel_id=1, source_target_pairs={{0,12},{2,14},{4,8},{6,10},{8,4},{10,6},{12,0},{14,2},{1,13},{3,15... | collective-permute-start | bytes 122888 | tf_op jit(solution)/shard_map/ppermute | solution.py:31
  39.3 0.2 collective-permute-start.12
  39.5 0.0 collective-permute-done.14.refs_1_
  39.5 1.4 %collective-permute-start.15 = (bf16[32,640]{1,0:T(8,128)(2,1)S(1)}, bf16[32,640]{1,0:T(8,128)(2,1)S(1)}, u32[]{:S(2)}, u32[]{:S(2)}) collective-permute-start(bf16[32,640]{1,0:T(8,128)(2,1)S(1)} %get-tuple-element.40), channel_id=1, source_target_pairs={{0,4},{2,6},{4,0},{6,2},{8,12},{10,14},{12,8},{14,10},{1,5},{3,7},... | collective-permute-start | bytes 122888 | tf_op jit(solution)/shard_map/ppermute | solution.py:31
  40.9 1.4 %collective-permute-done.11 = bf16[32,640]{1,0:T(8,128)(2,1)S(1)} collective-permute-done((bf16[32,640]{1,0:T(8,128)(2,1)S(1)}, bf16[32,640]{1,0:T(8,128)(2,1)S(1)}, u32[]{:S(2)}, u32[]{:S(2)}) %collective-permute-start.11) | collective-permute-done | bytes 40992 | tf_op jit(solution)/shard_map/ppermute | solution.py:31
  42.4 1.8 %collective-permute-done.12 = bf16[32,640]{1,0:T(8,128)(2,1)S(1)} collective-permute-done((bf16[32,640]{1,0:T(8,128)(2,1)S(1)}, bf16[32,640]{1,0:T(8,128)(2,1)S(1)}, u32[]{:S(2)}, u32[]{:S(2)}) %collective-permute-start.12) | collective-permute-done | bytes 40992 | tf_op jit(solution)/shard_map/ppermute | solution.py:31
  44.2 0.0 collective-permute-done.15
  44.2 0.0 copy-done.4
  44.2 0.7 %fusion = bf16[640,32]{0,1:T(8,128)(2,1)} fusion(bf16[32,640]{1,0:T(8,128)(2,1)S(1)} %collective-permute-done.15, f32[32,640]{1,0:T(8,128)S(1)} %get-tuple-element.39, bf16[32,640]{1,0:T(8,128)(2,1)S(1)} %collective-permute-done.12, bf16[32,640]{1,0:T(8,128)(2,1)S(1)} %collective-permute-done.11, f32[640]{0:T(1024)S(1)} %copy-done.4, ...), kind=kLoop, calls=%fused_computation.1 | loop fusion | flops 204800 | bytes 289280 | tf_op jit(solution)/shard_map/transpose | solution.py:419
  (10 shorter events, 0.1 us)
Async XLA Ops:
  0.0 7.4 %collective-permute-start.1 = (bf16[32,640]{1,0:T(8,128)(2,1)}, bf16[32,640]{1,0:T(8,128)(2,1)S(1)}, u32[]{:S(2)}, u32[]{:S(2)}) collective-permute-start(bf16[32,640]{1,0:T(8,128)(2,1)} %bitcast.8), channel_id=1, source_target_pairs={{0,8},{2,10},{4,12},{6,14},{8,0},{10,2},{12,4},{14,6},{1,9},{3,11}... | collective-permute-start | bytes 122888 | tf_op jit(solution)/shard_map/ppermute | solution.py:31
  4.1 4.2 %collective-permute-start = (bf16[32,640]{1,0:T(8,128)(2,1)}, bf16[32,640]{1,0:T(8,128)(2,1)S(1)}, u32[]{:S(2)}, u32[]{:S(2)}) collective-permute-start(bf16[32,640]{1,0:T(8,128)(2,1)} %bitcast.9), channel_id=1, source_target_pairs={{0,4},{2,6},{4,0},{6,2},{8,12},{10,14},{12,8},{14,10},{1,5},{3,7},... | collective-permute-start | bytes 122888 | tf_op jit(solution)/shard_map/ppermute | solution.py:31
  5.6 6.0 %collective-permute-start.2 = (bf16[32,640]{1,0:T(8,128)(2,1)}, bf16[32,640]{1,0:T(8,128)(2,1)S(1)}, u32[]{:S(2)}, u32[]{:S(2)}) collective-permute-start(bf16[32,640]{1,0:T(8,128)(2,1)} %bitcast.10), channel_id=1, source_target_pairs={{0,12},{2,14},{4,8},{6,10},{8,4},{10,6},{12,0},{14,2},{1,13},{3,15... | collective-permute-start | bytes 122888 | tf_op jit(solution)/shard_map/ppermute | solution.py:31
  5.6 7.5 %collective-permute-start.3 = (bf16[32,640]{1,0:T(8,128)(2,1)}, bf16[32,640]{1,0:T(8,128)(2,1)S(1)}, u32[]{:S(2)}, u32[]{:S(2)}) collective-permute-start(bf16[32,640]{1,0:T(8,128)(2,1)} %bitcast.11), channel_id=1, source_target_pairs={{0,2},{2,0},{4,6},{6,4},{8,10},{10,8},{12,14},{14,12},{1,3},{3,1},... | collective-permute-start | bytes 122888 | tf_op jit(solution)/shard_map/ppermute | solution.py:31
  8.3 7.4 %slice-start.5 = ((s8[5242880]{0:T(1024)(128)(4,1)}), s8[4194304]{0:T(1024)(128)(4,1)S(1)}, s32[]{:S(2)}) async-start(s8[5242880]{0:T(1024)(128)(4,1)} %bitcast.6), calls=%async_computation.5 | async-start | bytes 8388608
  8.3 7.5 %slice-start = ((s8[20971520]{0:T(1024)(128)(4,1)}), s8[4194304]{0:T(1024)(128)(4,1)S(1)}, s32[]{:S(2)}) async-start(s8[20971520]{0:T(1024)(128)(4,1)} %bitcast.4), calls=%async_computation | async-start | bytes 8388608
  8.3 7.4 %slice-start.6 = ((s8[5242880]{0:T(1024)(128)(4,1)}), s8[1048576]{0:T(1024)(128)(4,1)S(1)}, s32[]{:S(2)}) async-start(s8[5242880]{0:T(1024)(128)(4,1)} %bitcast.6), calls=%async_computation.6 | async-start | bytes 2097152
  8.3 7.4 %copy-start.2 = (bf16[640,32]{0,1:T(8,128)(2,1)S(1)}, bf16[640,32]{0,1:T(8,128)(2,1)}, u32[]{:S(2)}) copy-start(bf16[640,32]{0,1:T(8,128)(2,1)} %param.7) | copy-start | bytes 122884
  8.3 7.5 %slice-start.1 = ((s8[20971520]{0:T(1024)(128)(4,1)}), s8[4194304]{0:T(1024)(128)(4,1)S(1)}, s32[]{:S(2)}) async-start(s8[20971520]{0:T(1024)(128)(4,1)} %bitcast.4), calls=%async_computation.1 | async-start | bytes 8388608
  8.3 7.5 %slice-start.2 = ((s8[20971520]{0:T(1024)(128)(4,1)}), s8[4194304]{0:T(1024)(128)(4,1)S(1)}, s32[]{:S(2)}) async-start(s8[20971520]{0:T(1024)(128)(4,1)} %bitcast.4), calls=%async_computation.2 | async-start | bytes 8388608
  8.3 7.5 %slice-start.3 = ((s8[20971520]{0:T(1024)(128)(4,1)}), s8[4194304]{0:T(1024)(128)(4,1)S(1)}, s32[]{:S(2)}) async-start(s8[20971520]{0:T(1024)(128)(4,1)} %bitcast.4), calls=%async_computation.3 | async-start | bytes 8388608
  8.4 8.5 %slice-start.4 = ((s8[20971520]{0:T(1024)(128)(4,1)}), s8[4194304]{0:T(1024)(128)(4,1)S(1)}, s32[]{:S(2)}) async-start(s8[20971520]{0:T(1024)(128)(4,1)} %bitcast.4), calls=%async_computation.4 | async-start | bytes 8388608
  8.4 7.3 %collective-permute-start.5 = (bf16[2,32,640]{2,1,0:T(8,128)(2,1)S(1)}, bf16[2,32,640]{2,1,0:T(8,128)(2,1)S(1)}, u32[]{:S(2)}, u32[]{:S(2)}) collective-permute-start(bf16[2,32,640]{2,1,0:T(8,128)(2,1)S(1)} %shard_map.74), channel_id=1, source_target_pairs={{0,2},{2,0},{4,6},{6,4},{8,10},{10,8},{12,14},{14,12},{1,3},{3,1},... | collective-permute-start | bytes 245768 | tf_op jit(solution)/shard_map/ppermute | solution.py:31
  11.7 4.0 %collective-permute-start.4 = (bf16[32,640]{1,0:T(8,128)(2,1)S(1)}, bf16[32,640]{1,0:T(8,128)(2,1)S(1)}, u32[]{:S(2)}, u32[]{:S(2)}) collective-permute-start(bf16[32,640]{1,0:T(8,128)(2,1)S(1)} %shard_map.73.refs_4_), channel_id=1, source_target_pairs={{0,2},{2,0},{4,6},{6,4},{8,10},{10,8},{12,14},{14,12},{1,3},{3,1},... | collective-permute-start | bytes 122888 | tf_op jit(solution)/shard_map/ppermute | solution.py:31
  15.7 2.0 %copy-start = (bf16[10,40,512]{2,1,0:T(8,128)(2,1)S(1)}, bf16[10,40,512]{2,1,0:T(8,128)(2,1)}, u32[]{:S(2)}) copy-start(bf16[10,40,512]{2,1,0:T(8,128)(2,1)} %refs_3_.7) | copy-start | bytes 1228804
  15.7 2.0 %collective-permute-start.6 = (bf16[8,32,640]{2,1,0:T(8,128)(2,1)S(1)}, bf16[8,32,640]{2,1,0:T(8,128)(2,1)S(1)}, u32[]{:S(2)}, u32[]{:S(2)}) collective-permute-start(bf16[8,32,640]{2,1,0:T(8,128)(2,1)S(1)} %shard_map.75.refs_0_), channel_id=1, source_target_pairs={{0,1},{1,0},{2,3},{3,2},{4,5},{5,4},{6,7},{7,6},{8,9},{9,8},{10,11... | collective-permute-start | bytes 983048 | tf_op jit(solution)/shard_map/ppermute | solution.py:31
  19.5 4.7 %collective-permute-start.8 = (bf16[3,32,512]{2,1,0:T(8,128)(2,1)S(1)}, bf16[3,32,512]{2,1,0:T(8,128)(2,1)S(1)}, u32[]{:S(2)}, u32[]{:S(2)}) collective-permute-start(bf16[3,32,512]{2,1,0:T(8,128)(2,1)S(1)} %get-tuple-element.28), channel_id=1, source_target_pairs={{0,16},{16,0},{1,17},{17,1},{2,18},{18,2},{3,19},{19,3},{4,20},{20... | collective-permute-start | bytes 294920 | tf_op jit(solution)/shard_map/ppermute | solution.py:31
  21.1 3.1 %copy-start.1 = (f32[10,512]{1,0:T(8,128)S(1)}, f32[10,512]{1,0:T(8,128)}, u32[]{:S(2)}) copy-start(f32[10,512]{1,0:T(8,128)} %refs_4_.7) | copy-start | bytes 61444
  21.1 3.1 %copy-start.3 = (s32[10]{0:T(128)S(1)}, s32[10]{0:T(128)}, u32[]{:S(2)}) copy-start(s32[10]{0:T(128)} %refs_0_.7) | copy-start | bytes 124
  22.7 4.7 %collective-permute-start.7 = (bf16[3,32,512]{2,1,0:T(8,128)(2,1)S(1)}, bf16[3,32,512]{2,1,0:T(8,128)(2,1)S(1)}, u32[]{:S(2)}, u32[]{:S(2)}) collective-permute-start(bf16[3,32,512]{2,1,0:T(8,128)(2,1)S(1)} %get-tuple-element.25.refs_6_), channel_id=1, source_target_pairs={{0,16},{16,0},{1,17},{17,1},{2,18},{18,2},{3,19},{19,3},{4,20},{20... | collective-permute-start | bytes 294920 | tf_op jit(solution)/shard_map/ppermute | solution.py:31
  29.0 1.5 %collective-permute-start.9 = (bf16[4,32,640]{2,1,0:T(8,128)(2,1)S(1)}, bf16[4,32,640]{2,1,0:T(8,128)(2,1)S(1)}, u32[]{:S(2)}, u32[]{:S(2)}) collective-permute-start(bf16[4,32,640]{2,1,0:T(8,128)(2,1)S(1)} %get-tuple-element.30), channel_id=1, source_target_pairs={{0,1},{1,0},{2,3},{3,2},{4,5},{5,4},{6,7},{7,6},{8,9},{9,8},{10,11... | collective-permute-start | bytes 491528 | tf_op jit(solution)/shard_map/ppermute | solution.py:31
  30.5 13.8 %copy-start.4 = (f32[640]{0:T(1024)S(1)}, f32[640]{0:T(1024)}, u32[]{:S(2)}) copy-start(f32[640]{0:T(1024)} %param.8) | copy-start | bytes 7684
  31.0 1.8 %collective-permute-start.13 = (bf16[4,32,640]{2,1,0:T(8,128)(2,1)S(1)}, bf16[4,32,640]{2,1,0:T(8,128)(2,1)S(1)}, u32[]{:S(2)}, u32[]{:S(2)}) collective-permute-start(bf16[4,32,640]{2,1,0:T(8,128)(2,1)S(1)} %get-tuple-element.36), channel_id=1, source_target_pairs={{0,1},{1,0},{2,3},{3,2},{4,5},{5,4},{6,7},{7,6},{8,9},{9,8},{10,11... | collective-permute-start | bytes 491528 | tf_op jit(solution)/shard_map/ppermute | solution.py:31
  31.3 5.1 %collective-permute-start.10 = (bf16[2,32,640]{2,1,0:T(8,128)(2,1)S(1)}, bf16[2,32,640]{2,1,0:T(8,128)(2,1)S(1)}, u32[]{:S(2)}, u32[]{:S(2)}) collective-permute-start(bf16[2,32,640]{2,1,0:T(8,128)(2,1)S(1)} %get-tuple-element.32), channel_id=1, source_target_pairs={{0,2},{2,0},{4,6},{6,4},{8,10},{10,8},{12,14},{14,12},{1,3},{3,1},... | collective-permute-start | bytes 245768 | tf_op jit(solution)/shard_map/ppermute | solution.py:31
  32.8 6.7 %collective-permute-start.14 = (bf16[2,32,640]{2,1,0:T(8,128)(2,1)S(1)}, bf16[2,32,640]{2,1,0:T(8,128)(2,1)S(1)}, u32[]{:S(2)}, u32[]{:S(2)}) collective-permute-start(bf16[2,32,640]{2,1,0:T(8,128)(2,1)S(1)} %get-tuple-element.38), channel_id=1, source_target_pairs={{0,2},{2,0},{4,6},{6,4},{8,10},{10,8},{12,14},{14,12},{1,3},{3,1},... | collective-permute-start | bytes 245768 | tf_op jit(solution)/shard_map/ppermute | solution.py:31
  36.4 6.0 %collective-permute-start.11 = (bf16[32,640]{1,0:T(8,128)(2,1)S(1)}, bf16[32,640]{1,0:T(8,128)(2,1)S(1)}, u32[]{:S(2)}, u32[]{:S(2)}) collective-permute-start(bf16[32,640]{1,0:T(8,128)(2,1)S(1)} %get-tuple-element.33), channel_id=1, source_target_pairs={{0,12},{2,14},{4,8},{6,10},{8,4},{10,6},{12,0},{14,2},{1,13},{3,15... | collective-permute-start | bytes 122888 | tf_op jit(solution)/shard_map/ppermute | solution.py:31
  39.3 4.9 %collective-permute-start.12 = (bf16[32,640]{1,0:T(8,128)(2,1)S(1)}, bf16[32,640]{1,0:T(8,128)(2,1)S(1)}, u32[]{:S(2)}, u32[]{:S(2)}) collective-permute-start(bf16[32,640]{1,0:T(8,128)(2,1)S(1)} %get-tuple-element.34), channel_id=1, source_target_pairs={{0,8},{2,10},{4,12},{6,14},{8,0},{10,2},{12,4},{14,6},{1,9},{3,11}... | collective-permute-start | bytes 122888 | tf_op jit(solution)/shard_map/ppermute | solution.py:31
  39.5 4.7 %collective-permute-start.15 = (bf16[32,640]{1,0:T(8,128)(2,1)S(1)}, bf16[32,640]{1,0:T(8,128)(2,1)S(1)}, u32[]{:S(2)}, u32[]{:S(2)}) collective-permute-start(bf16[32,640]{1,0:T(8,128)(2,1)S(1)} %get-tuple-element.40), channel_id=1, source_target_pairs={{0,4},{2,6},{4,0},{6,2},{8,12},{10,14},{12,8},{14,10},{1,5},{3,7},... | collective-permute-start | bytes 122888 | tf_op jit(solution)/shard_map/ppermute | solution.py:31

commit v2 on v0

--- a/solution.py
+++ b/solution.py
@@ -76,12 +76,6 @@
             self.parts = [(0,)]
             self.run = self.occs
 
-        if 2 * self.aux <= self.points and self.aux % LANES == 0:
-            self.packed = [(0, 0), (0, self.aux)]
-        else:
-            self.packed = [(0, 0), (1, 0)]
-        self.slots = self.packed[-1][0] + 1
-
     def masks(self, part):
         if len(self.parts) == 1:
             return list(range(self.count))
@@ -163,19 +157,6 @@
             half[m], factor_block(plan, fac, m, plan.part(h)), NT, preferred_element_type=jnp.float32
         )
     refs[-1][...] = value
-
-
-def second_dens_kernel(plan, span, rows, vir, occ, other, fac, part, dens, sent, total, occ32):
-    dens_kernel(plan, span, rows, vir, occ, dens, sent, occ32)
-    fac_kernel(plan, 1, other, fac, part, total)
-    value = total[...]
-    if 2 * plan.aux < plan.slots * plan.points:
-        for slot in range(plan.slots):
-            sent[len(span) + slot] = jnp.zeros(sent.shape[1:], sent.dtype)
-    for slot, lane in plan.packed:
-        term = value.astype(sent.dtype)
-        sent[len(span) + slot, :, lane : lane + plan.aux] = term
-        value = value - term.astype(jnp.float32)
 
 
 def grid_kernel(plan, part, span, skip, live, dens_a, dens_b, occ, weight, vir, *refs):
@@ -203,11 +184,7 @@
 
 
 def back_kernel(plan, part, part_a, part_b, fac, acc, stay, sent):
-    both = part_a[...]
-    first = part_b.shape[0] - plan.slots
-    for slot, lane in plan.packed:
-        both = both + part_b[first + slot, :, lane : lane + plan.aux].astype(jnp.float32)
-    both = both.astype(jnp.bfloat16)
+    both = (part_a[...] + part_b[...]).astype(jnp.bfloat16)
     k, tiles = plan.k, plan.virs // LANES
     masks = plan.masks(part)
     for n, m in enumerate(masks):
@@ -305,18 +282,18 @@
         [occ_scratch(spans[0])],
     )(mine, other, vir_values, occ_values, part)
     first_other = swap(sent, "grp", groups, 1)
-    second_dens, sent, part = call(
-        bind(second_dens_kernel, spans[1]),
-        (
-            shape(chunks[1], f32),
-            shape((len(spans[1]) + plan.slots, k, points), bf16),
-            shape((k, plan.aux), f32),
-        ),
-        [VMEM] * 6,
-        grid_flops * len(spans[1]) + flops,
+    second_dens, sent = call(
+        bind(dens_kernel, spans[1]),
+        (shape(chunks[1], f32), shape(chunks[1], bf16)),
+        [VMEM] * 3,
+        grid_flops * len(spans[1]),
         [occ_scratch(spans[1])],
-    )(rows, vir_values, occ_values, other, coulomb_factors, part)
+    )(rows, vir_values, occ_values)
     second_other = swap(sent, "grp", groups, 1)
+    part = call(
+        after(bind(fac_kernel, 1), 2), shape((k, plan.aux), f32), [VMEM] * 2 + [ANY, VMEM], flops
+    )(other, coulomb_factors, sent, part)
+    other_part = swap(part, "grp", groups, 1)
 
     def grid(chosen, chunk, dens, came, skip, *more):
         used = plan.run * len(chosen)
@@ -331,7 +308,7 @@
         )(live_points, dens, came, occ_values, kernel, vir_values, *more)
 
     every = sum(plan.parts, ())
-    begun = grid(every, 0, first_dens, first_other, None, sent)
+    begun = grid(every, 0, first_dens, first_other, None, part)
 
     def finish(number, *order):
         skip = sum(len(chosen) for chosen in plan.parts[:number]) * plan.run * k
@@ -346,7 +323,7 @@
             (shape(share, f32), shape(share, bf16)),
             [VMEM] * 4 + [ANY] * len(order),
             2 * flops // len(plan.parts),
-        )(part, second_other, coulomb_factors, acc, *order)
+        )(part, other_part, coulomb_factors, acc, *order)
 
     if len(plan.parts) == 2:
         (stride, radix), (top, _) = digits

time: 43.7 us -> 43.1 us (0.986)
  waiting for transfers between devices: 14.5 us -> 12.2 us
  starting transfers between devices: 18.9 us -> 20.4 us
    ppermute x17 -> x18, waiting for transfers between devices: 14.5 us -> 12.2 us  [swap(): return lax.ppermute(x, axis, [(i, i ^ mask) for i in range(count)])]
    ppermute x17 -> x18, starting transfers between devices: 18.9 us -> 20.4 us  [swap(): return lax.ppermute(x, axis, [(i, i ^ mask) for i in range(count)])]
    pallas_call x1 -> x2, Pallas kernels: 1.59 us -> 1.73 us  [the longest x1 0.88 us: local(): call(bind(dens_kernel, spans[1]), (shape(chunks[1], f32), shape(chunks[1]...]
  transfers between devices with their start and end apart: 17 -> 18, of which waited for: 11 -> 9; matrix products, arithmetic and copies ran while one was open for 0% -> 0% of each run, Pallas kernels for 12% -> 15%
where the time goes in v2:
time: 43.1 us; the launch traced here: 43 us
  starting transfers between devices  20.4 us (47%)
  waiting for transfers between devices  12.2 us (28%)
  Pallas kernels  9.41 us (22%)
  other arithmetic  0.65 us (2%)
    ppermute x18, starting transfers between devices, swap(): return lax.ppermute(x, axis, [(i, i ^ mask) for i in range(count)])  20.4 us
    ppermute x18, waiting for transfers between devices, swap(): return lax.ppermute(x, axis, [(i, i ^ mask) for i in range(count)])  12.2 us
    pallas_call x3, Pallas kernels, grid(): call(after(body, count) if len(more) + 6 > count else body, shape((used *...  3.83 us
    pallas_call x1, Pallas kernels, local(): call(after(bind(first_dens_kernel, spans[0]), 4), (shape(chunks[0], f32),...  1.78 us
    pallas_call x2, Pallas kernels, back(): call(after(body, 4) if order else body, (shape(share, f32), shape(share,...  1.07 us
    pallas_call x1, Pallas kernels, local(): call(bind(dens_kernel, spans[1]), (shape(chunks[1], f32), shape(chunks[1]...  0.88 us
    pallas_call x1, Pallas kernels, local(): call(bind(fac_kernel, 0), shape((k, plan.aux), f32), [VMEM] * 2, flops)  0.87 us
  transfers between devices with their start and end apart: 18, of which 9 were waited for; matrix products, arithmetic and copies ran while one was open for 0% of the time, Pallas kernels for 15%

profile of v2, /device:TPU:0, one launch (start us, length us, event | category | flops | bytes accessed | tf_op | source)
XLA Modules:
  0.0 43.0 jit_solution(1483753645028205468)
XLA Ops:
  0.0 0.0 slice-start.2
  0.0 0.0 slice-start.3
  0.0 0.0 slice-start.4
  0.0 5.2 %collective-permute-start.5 = (bf16[32,640]{1,0:T(8,128)(2,1)}, bf16[32,640]{1,0:T(8,128)(2,1)S(1)}, u32[]{:S(2)}, u32[]{:S(2)}) collective-permute-start(bf16[32,640]{1,0:T(8,128)(2,1)} %bitcast.8), channel_id=1, source_target_pairs={{0,12},{2,14},{4,8},{6,10},{8,4},{10,6},{12,0},{14,2},{1,13},{3,15... | collective-permute-start | bytes 122888 | tf_op jit(solution)/shard_map/ppermute | solution.py:31
  5.2 0.0 collective-permute-start.3
  5.2 0.6 %collective-permute-start.1 = (bf16[32,640]{1,0:T(8,128)(2,1)}, bf16[32,640]{1,0:T(8,128)(2,1)S(1)}, u32[]{:S(2)}, u32[]{:S(2)}) collective-permute-start(bf16[32,640]{1,0:T(8,128)(2,1)} %bitcast.10), channel_id=1, source_target_pairs={{0,4},{2,6},{4,0},{6,2},{8,12},{10,14},{12,8},{14,10},{1,5},{3,7},... | collective-permute-start | bytes 122888 | tf_op jit(solution)/shard_map/ppermute | solution.py:31
  5.8 1.7 %collective-permute-start = (bf16[32,640]{1,0:T(8,128)(2,1)}, bf16[32,640]{1,0:T(8,128)(2,1)S(1)}, u32[]{:S(2)}, u32[]{:S(2)}) collective-permute-start(bf16[32,640]{1,0:T(8,128)(2,1)} %bitcast.11), channel_id=1, source_target_pairs={{0,2},{2,0},{4,6},{6,4},{8,10},{10,8},{12,14},{14,12},{1,3},{3,1},... | collective-permute-start | bytes 122888 | tf_op jit(solution)/shard_map/ppermute | solution.py:31
  7.5 0.0 collective-permute-done.5.refs_0_
  7.5 1.8 %collective-permute-start.6 = (bf16[32,640]{1,0:T(8,128)(2,1)S(1)}, bf16[32,640]{1,0:T(8,128)(2,1)S(1)}, u32[]{:S(2)}, u32[]{:S(2)}) collective-permute-start(bf16[32,640]{1,0:T(8,128)(2,1)S(1)} %shard_map.73.refs_7_), channel_id=1, source_target_pairs={{0,2},{2,0},{4,6},{6,4},{8,10},{10,8},{12,14},{14,12},{1,3},{3,1},... | collective-permute-start | bytes 122888 | tf_op jit(solution)/shard_map/ppermute | solution.py:31
  9.3 1.0 %collective-permute-done.3.refs_5_ = bf16[32,640]{1,0:T(8,128)(2,1)S(1)} collective-permute-done((bf16[32,640]{1,0:T(8,128)(2,1)}, bf16[32,640]{1,0:T(8,128)(2,1)S(1)}, u32[]{:S(2)}, u32[]{:S(2)}) %collective-permute-start.3) | collective-permute-done | bytes 40992 | tf_op jit(solution)/shard_map/ppermute | solution.py:31
  10.3 1.5 %collective-permute-start.4 = (bf16[32,640]{1,0:T(8,128)(2,1)S(1)}, bf16[32,640]{1,0:T(8,128)(2,1)S(1)}, u32[]{:S(2)}, u32[]{:S(2)}) collective-permute-start(bf16[32,640]{1,0:T(8,128)(2,1)S(1)} %collective-permute-done.3.refs_5_), channel_id=1, source_target_pairs={{0,2},{2,0},{4,6},{6,4},{8,10},{10,8},{12,14},{14,12},{1,3},{3,1},... | collective-permute-start | bytes 122888 | tf_op jit(solution)/shard_map/ppermute | solution.py:31
  11.8 0.0 collective-permute-done.1.refs_3_
  11.8 0.5 %collective-permute-start.2 = (bf16[32,640]{1,0:T(8,128)(2,1)S(1)}, bf16[32,640]{1,0:T(8,128)(2,1)S(1)}, u32[]{:S(2)}, u32[]{:S(2)}) collective-permute-start(bf16[32,640]{1,0:T(8,128)(2,1)S(1)} %collective-permute-done.1.refs_3_), channel_id=1, source_target_pairs={{0,2},{2,0},{4,6},{6,4},{8,10},{10,8},{12,14},{14,12},{1,3},{3,1},... | collective-permute-start | bytes 122888 | tf_op jit(solution)/shard_map/ppermute | solution.py:31
  12.3 0.0 collective-permute-done.refs_2_
  12.4 0.0 collective-permute-done.6.refs_8_
  12.4 2.0 %collective-permute-done.4.refs_6_ = bf16[32,640]{1,0:T(8,128)(2,1)S(1)} collective-permute-done((bf16[32,640]{1,0:T(8,128)(2,1)S(1)}, bf16[32,640]{1,0:T(8,128)(2,1)S(1)}, u32[]{:S(2)}, u32[]{:S(2)}) %collective-permute-start.4) | collective-permute-done | bytes 40992 | tf_op jit(solution)/shard_map/ppermute | solution.py:31
  14.3 1.5 %collective-permute-done.2.refs_4_ = bf16[32,640]{1,0:T(8,128)(2,1)S(1)} collective-permute-done((bf16[32,640]{1,0:T(8,128)(2,1)S(1)}, bf16[32,640]{1,0:T(8,128)(2,1)S(1)}, u32[]{:S(2)}, u32[]{:S(2)}) %collective-permute-start.2) | collective-permute-done | bytes 40992 | tf_op jit(solution)/shard_map/ppermute | solution.py:31
  15.8 0.0 slice-done.5
  15.8 0.0 slice-done.6
  15.8 0.0 copy-done.2
  15.9 0.0 copy-start
  15.9 0.1 collective-permute-start.7
  16.0 0.0 slice-done
  16.0 0.0 slice-done.1
  16.0 0.0 slice-done.2
  16.0 0.0 slice-done.3
  16.0 0.0 slice-done.4
  16.0 0.9 %shard_map.75.refs_4_.refs_3_ = f32[32,256]{1,0:T(8,128)S(1)} custom-call(bf16[8,32,640]{2,1,0:T(8,128)(2,1)S(1)} %shard_map.74.refs_0_, bf16[512,20480]{1,0:T(8,128)(2,1)S(1)} %bitcast.5), custom_call_target="tpu_custom_call" | custom-call | flops 83886080 | tf_op jit(solution)/shard_map/pallas_call | solution.py:265
  16.9 0.7 %collective-permute-done.7.refs_1_.refs_0_ = bf16[8,32,640]{2,1,0:T(8,128)(2,1)S(1)} collective-permute-done((bf16[8,32,640]{2,1,0:T(8,128)(2,1)S(1)}, bf16[8,32,640]{2,1,0:T(8,128)(2,1)S(1)}, u32[]{:S(2)}, u32[]{:S(2)}) %collective-permute-start.7) | collective-permute-done | bytes 327712 | tf_op jit(solution)/shard_map/ppermute | solution.py:31
  17.6 0.0 copy-done
  17.6 1.8 %shard_map.76 = (f32[3,32,512]{2,1,0:T(8,128)S(1)}, bf16[3,32,512]{2,1,0:T(8,128)(2,1)S(1)}, bf16[640,512]{1,0:T(8,128)(2,1)S(1)}) custom-call(bf16[8,32,640]{2,1,0:T(8,128)(2,1)S(1)} %shard_map.74.refs_0_, bf16[8,32,640]{2,1,0:T(8,128)(2,1)S(1)} %collective-permute-done.7.refs_1_.refs_0_, bf16[10,512,512]{2,1,0:T(8,128)(2,1)S(1)} %bitcast.7, ...), custom_call_target="tpu_custom_call" | custom-call | flops 1006632960 | tf_op jit(solution)/shard_map/pallas_call | solution.py:277
  19.4 1.6 %collective-permute-start.10 = (bf16[3,32,512]{2,1,0:T(8,128)(2,1)S(1)}, bf16[3,32,512]{2,1,0:T(8,128)(2,1)S(1)}, u32[]{:S(2)}, u32[]{:S(2)}) collective-permute-start(bf16[3,32,512]{2,1,0:T(8,128)(2,1)S(1)} %get-tuple-element.26), channel_id=1, source_target_pairs={{0,16},{16,0},{1,17},{17,1},{2,18},{18,2},{3,19},{19,3},{4,20},{20... | collective-permute-start | bytes 294920 | tf_op jit(solution)/shard_map/ppermute | solution.py:31
  21.0 0.9 %shard_map.77 = (f32[2,32,512]{2,1,0:T(8,128)S(1)}, bf16[2,32,512]{2,1,0:T(8,128)(2,1)S(1)}) custom-call(bf16[640,512]{1,0:T(8,128)(2,1)S(1)} %get-tuple-element.22.refs_0_, bf16[10,512,512]{2,1,0:T(8,128)(2,1)S(1)} %bitcast.7, bf16[10,40,512]{2,1,0:T(8,128)(2,1)S(1)} %copy-done), custom_call_target="tpu_custom_call" | custom-call | flops 671088640 | tf_op jit(solution)/shard_map/pallas_call | solution.py:285
  21.8 0.0 copy-start.1
  21.9 0.0 copy-start.3
  21.9 0.6 %collective-permute-start.9 = (bf16[2,32,512]{2,1,0:T(8,128)(2,1)S(1)}, bf16[2,32,512]{2,1,0:T(8,128)(2,1)S(1)}, u32[]{:S(2)}, u32[]{:S(2)}) collective-permute-start(bf16[2,32,512]{2,1,0:T(8,128)(2,1)S(1)} %get-tuple-element.23.refs_2_), channel_id=1, source_target_pairs={{0,16},{16,0},{1,17},{17,1},{2,18},{18,2},{3,19},{19,3},{4,20},{20... | collective-permute-start | bytes 196616 | tf_op jit(solution)/shard_map/ppermute | solution.py:31
  22.5 0.8 %shard_map.78.refs_6_.refs_0_ = f32[32,256]{1,0:T(8,128)S(1)} custom-call(bf16[8,32,640]{2,1,0:T(8,128)(2,1)S(1)} %collective-permute-done.7.refs_1_.refs_0_, bf16[512,20480]{1,0:T(8,128)(2,1)S(1)} %bitcast.5, bf16[2,32,512]{2,1,0:T(8,128)(2,1)S(1)} %get-tuple-element.23.refs_2_, f32[32,256]{1,0:T(8,128)S(1)} %shard_map.75.refs_4_.refs_3_), custom_call_target="tpu_custom_call" | custom-call | flops 83886080 | tf_op jit(solution)/shard_map/pallas_call | solution.py:293
  23.3 1.5 %collective-permute-start.8 = (f32[32,256]{1,0:T(8,128)S(1)}, f32[32,256]{1,0:T(8,128)S(1)}, u32[]{:S(2)}, u32[]{:S(2)}) collective-permute-start(f32[32,256]{1,0:T(8,128)S(1)} %shard_map.78.refs_6_.refs_0_), channel_id=1, source_target_pairs={{0,16},{16,0},{1,17},{17,1},{2,18},{18,2},{3,19},{19,3},{4,20},{20... | collective-permute-start | bytes 98312 | tf_op jit(solution)/shard_map/ppermute | solution.py:31
  24.9 0.0 collective-permute-done.10.refs_2_
  24.9 0.0 copy-done.3
  24.9 1.7 %shard_map.79.refs_6_ = f32[640,512]{1,0:T(8,128)S(1)} custom-call(s32[10]{0:T(128)S(1)} %copy-done.3, f32[3,32,512]{2,1,0:T(8,128)S(1)} %get-tuple-element.25.refs_1_, bf16[3,32,512]{2,1,0:T(8,128)(2,1)S(1)} %collective-permute-done.10.refs_2_, bf16[10,40,512]{2,1,0:T(8,128)(2,1)S(1)} %copy-done, f32[10,512]{1,0:T(8,128)S(1)} %copy-done.1, ...), custom_call_target="tpu_custom_call" | custom-call | flops 1006632960 | tf_op jit(solution)/shard_map/pallas_call | solution.py:302
  26.6 0.0 collective-permute-done.9.refs_2_
  26.6 1.1 %shard_map.80.refs_3_ = f32[320,512]{1,0:T(8,128)S(1)} custom-call(s32[10]{0:T(128)S(1)} %copy-done.3, f32[2,32,512]{2,1,0:T(8,128)S(1)} %get-tuple-element.24.refs_1_, bf16[2,32,512]{2,1,0:T(8,128)(2,1)S(1)} %collective-permute-done.9.refs_2_, bf16[10,40,512]{2,1,0:T(8,128)(2,1)S(1)} %copy-done, f32[10,512]{1,0:T(8,128)S(1)} %copy-done.1, ...), custom_call_target="tpu_custom_call" | custom-call | flops 335544320 | tf_op jit(solution)/shard_map/pallas_call | solution.py:302
  27.7 0.0 collective-permute-done.8.refs_1_
  27.7 0.5 %shard_map.81 = (f32[4,32,640]{2,1,0:T(8,128)S(1)}, bf16[4,32,640]{2,1,0:T(8,128)(2,1)S(1)}) custom-call(f32[32,256]{1,0:T(8,128)S(1)} %shard_map.78.refs_6_.refs_0_, f32[32,256]{1,0:T(8,128)S(1)} %collective-permute-done.8.refs_1_, bf16[512,20480]{1,0:T(8,128)(2,1)S(1)} %bitcast.5, f32[320,512]{1,0:T(8,128)S(1)} %shard_map.80.refs_3_), custom_call_target="tpu_custom_call" | custom-call | flops 83886080 | tf_op jit(solution)/shard_map/pallas_call | solution.py:321
  28.2 0.1 collective-permute-start.11
  28.3 1.0 %shard_map.82.refs_2_.refs_3_ = f32[320,512]{1,0:T(8,128)S(1)} custom-call(s32[10]{0:T(128)S(1)} %copy-done.3, f32[2,32,512]{2,1,0:T(8,128)S(1)} %get-tuple-element.24.refs_1_, bf16[2,32,512]{2,1,0:T(8,128)(2,1)S(1)} %collective-permute-done.9.refs_2_, bf16[10,40,512]{2,1,0:T(8,128)(2,1)S(1)} %copy-done, f32[10,512]{1,0:T(8,128)S(1)} %copy-done.1, ...), custom_call_target="tpu_custom_call" | custom-call | flops 335544320 | tf_op jit(solution)/shard_map/pallas_call | solution.py:302
  29.4 0.3 collective-permute-done.11.refs_1_
  29.7 0.0 copy-start.4
  29.7 0.5 %shard_map.85 = (f32[4,32,640]{2,1,0:T(8,128)S(1)}, bf16[4,32,640]{2,1,0:T(8,128)(2,1)S(1)}) custom-call(f32[32,256]{1,0:T(8,128)S(1)} %shard_map.78.refs_6_.refs_0_, f32[32,256]{1,0:T(8,128)S(1)} %collective-permute-done.8.refs_1_, bf16[512,20480]{1,0:T(8,128)(2,1)S(1)} %bitcast.5, f32[320,512]{1,0:T(8,128)S(1)} %shard_map.82.refs_2_.refs_3_, ...), custom_call_target="tpu_custom_call" | custom-call | flops 83886080 | tf_op jit(solution)/shard_map/pallas_call | solution.py:321
  30.3 0.3 collective-permute-start.15
  30.5 0.5 %collective-permute-start.12 = (bf16[2,32,640]{2,1,0:T(8,128)(2,1)S(1)}, bf16[2,32,640]{2,1,0:T(8,128)(2,1)S(1)}, u32[]{:S(2)}, u32[]{:S(2)}) collective-permute-start(bf16[2,32,640]{2,1,0:T(8,128)(2,1)S(1)} %get-tuple-element.30), channel_id=1, source_target_pairs={{0,2},{2,0},{4,6},{6,4},{8,10},{10,8},{12,14},{14,12},{1,3},{3,1},... | collective-permute-start | bytes 245768 | tf_op jit(solution)/shard_map/ppermute | solution.py:31
  31.0 0.7 %collective-permute-done.15.refs_1_ = bf16[4,32,640]{2,1,0:T(8,128)(2,1)S(1)} collective-permute-done((bf16[4,32,640]{2,1,0:T(8,128)(2,1)S(1)}, bf16[4,32,640]{2,1,0:T(8,128)(2,1)S(1)}, u32[]{:S(2)}, u32[]{:S(2)}) %collective-permute-start.15) | collective-permute-done | bytes 163872 | tf_op jit(solution)/shard_map/ppermute | solution.py:31
  31.8 0.9 %collective-permute-start.16 = (bf16[2,32,640]{2,1,0:T(8,128)(2,1)S(1)}, bf16[2,32,640]{2,1,0:T(8,128)(2,1)S(1)}, u32[]{:S(2)}, u32[]{:S(2)}) collective-permute-start(bf16[2,32,640]{2,1,0:T(8,128)(2,1)S(1)} %get-tuple-element.36), channel_id=1, source_target_pairs={{0,2},{2,0},{4,6},{6,4},{8,10},{10,8},{12,14},{14,12},{1,3},{3,1},... | collective-permute-start | bytes 245768 | tf_op jit(solution)/shard_map/ppermute | solution.py:31
  32.7 3.1 %collective-permute-done.12.refs_1_ = bf16[2,32,640]{2,1,0:T(8,128)(2,1)S(1)} collective-permute-done((bf16[2,32,640]{2,1,0:T(8,128)(2,1)S(1)}, bf16[2,32,640]{2,1,0:T(8,128)(2,1)S(1)}, u32[]{:S(2)}, u32[]{:S(2)}) %collective-permute-start.12) | collective-permute-done | bytes 81952 | tf_op jit(solution)/shard_map/ppermute | solution.py:31
  35.8 0.6 %collective-permute-start.13 = (bf16[32,640]{1,0:T(8,128)(2,1)S(1)}, bf16[32,640]{1,0:T(8,128)(2,1)S(1)}, u32[]{:S(2)}, u32[]{:S(2)}) collective-permute-start(bf16[32,640]{1,0:T(8,128)(2,1)S(1)} %get-tuple-element.31), channel_id=1, source_target_pairs={{0,8},{2,10},{4,12},{6,14},{8,0},{10,2},{12,4},{14,6},{1,9},{3,11}... | collective-permute-start | bytes 122888 | tf_op jit(solution)/shard_map/ppermute | solution.py:31
  36.4 1.4 %collective-permute-start.14 = (bf16[32,640]{1,0:T(8,128)(2,1)S(1)}, bf16[32,640]{1,0:T(8,128)(2,1)S(1)}, u32[]{:S(2)}, u32[]{:S(2)}) collective-permute-start(bf16[32,640]{1,0:T(8,128)(2,1)S(1)} %get-tuple-element.32), channel_id=1, source_target_pairs={{0,12},{2,14},{4,8},{6,10},{8,4},{10,6},{12,0},{14,2},{1,13},{3,15... | collective-permute-start | bytes 122888 | tf_op jit(solution)/shard_map/ppermute | solution.py:31
  37.8 0.0 collective-permute-done.16.refs_1_
  37.8 1.6 %collective-permute-start.17 = (bf16[32,640]{1,0:T(8,128)(2,1)S(1)}, bf16[32,640]{1,0:T(8,128)(2,1)S(1)}, u32[]{:S(2)}, u32[]{:S(2)}) collective-permute-start(bf16[32,640]{1,0:T(8,128)(2,1)S(1)} %get-tuple-element.38), channel_id=1, source_target_pairs={{0,4},{2,6},{4,0},{6,2},{8,12},{10,14},{12,8},{14,10},{1,5},{3,7},... | collective-permute-start | bytes 122888 | tf_op jit(solution)/shard_map/ppermute | solution.py:31
  39.4 1.3 %collective-permute-done.13 = bf16[32,640]{1,0:T(8,128)(2,1)S(1)} collective-permute-done((bf16[32,640]{1,0:T(8,128)(2,1)S(1)}, bf16[32,640]{1,0:T(8,128)(2,1)S(1)}, u32[]{:S(2)}, u32[]{:S(2)}) %collective-permute-start.13) | collective-permute-done | bytes 40992 | tf_op jit(solution)/shard_map/ppermute | solution.py:31
  40.7 1.6 %collective-permute-done.14 = bf16[32,640]{1,0:T(8,128)(2,1)S(1)} collective-permute-done((bf16[32,640]{1,0:T(8,128)(2,1)S(1)}, bf16[32,640]{1,0:T(8,128)(2,1)S(1)}, u32[]{:S(2)}, u32[]{:S(2)}) %collective-permute-start.14) | collective-permute-done | bytes 40992 | tf_op jit(solution)/shard_map/ppermute | solution.py:31
  42.3 0.0 collective-permute-done.17
  42.3 0.0 copy-done.4
  42.3 0.7 %fusion = bf16[640,32]{0,1:T(8,128)(2,1)} fusion(bf16[32,640]{1,0:T(8,128)(2,1)S(1)} %collective-permute-done.17, f32[32,640]{1,0:T(8,128)S(1)} %get-tuple-element.37, bf16[32,640]{1,0:T(8,128)(2,1)S(1)} %collective-permute-done.14, bf16[32,640]{1,0:T(8,128)(2,1)S(1)} %collective-permute-done.13, f32[640]{0:T(1024)S(1)} %copy-done.4, ...), kind=kLoop, calls=%fused_computation.1 | loop fusion | flops 204800 | bytes 289280 | tf_op jit(solution)/shard_map/transpose | solution.py:375
  (14 shorter events, 0.2 us)
Async XLA Ops:
  0.0 15.8 %slice-start.5 = ((s8[5242880]{0:T(1024)(128)(4,1)}), s8[4194304]{0:T(1024)(128)(4,1)S(1)}, s32[]{:S(2)}) async-start(s8[5242880]{0:T(1024)(128)(4,1)} %bitcast.6), calls=%async_computation.5 | async-start | bytes 8388608
  0.0 16.0 %slice-start = ((s8[20971520]{0:T(1024)(128)(4,1)}), s8[4194304]{0:T(1024)(128)(4,1)S(1)}, s32[]{:S(2)}) async-start(s8[20971520]{0:T(1024)(128)(4,1)} %bitcast.4), calls=%async_computation | async-start | bytes 8388608
  0.0 15.8 %slice-start.6 = ((s8[5242880]{0:T(1024)(128)(4,1)}), s8[1048576]{0:T(1024)(128)(4,1)S(1)}, s32[]{:S(2)}) async-start(s8[5242880]{0:T(1024)(128)(4,1)} %bitcast.6), calls=%async_computation.6 | async-start | bytes 2097152
  0.0 15.8 %copy-start.2 = (bf16[640,32]{0,1:T(8,128)(2,1)S(1)}, bf16[640,32]{0,1:T(8,128)(2,1)}, u32[]{:S(2)}) copy-start(bf16[640,32]{0,1:T(8,128)(2,1)} %param.7) | copy-start | bytes 122884
  0.0 16.0 %slice-start.1 = ((s8[20971520]{0:T(1024)(128)(4,1)}), s8[4194304]{0:T(1024)(128)(4,1)S(1)}, s32[]{:S(2)}) async-start(s8[20971520]{0:T(1024)(128)(4,1)} %bitcast.4), calls=%async_computation.1 | async-start | bytes 8388608
  0.0 16.0 %slice-start.2 = ((s8[20971520]{0:T(1024)(128)(4,1)}), s8[4194304]{0:T(1024)(128)(4,1)S(1)}, s32[]{:S(2)}) async-start(s8[20971520]{0:T(1024)(128)(4,1)} %bitcast.4), calls=%async_computation.2 | async-start | bytes 8388608
  0.0 16.0 %slice-start.3 = ((s8[20971520]{0:T(1024)(128)(4,1)}), s8[4194304]{0:T(1024)(128)(4,1)S(1)}, s32[]{:S(2)}) async-start(s8[20971520]{0:T(1024)(128)(4,1)} %bitcast.4), calls=%async_computation.3 | async-start | bytes 8388608
  0.0 16.0 %slice-start.4 = ((s8[20971520]{0:T(1024)(128)(4,1)}), s8[4194304]{0:T(1024)(128)(4,1)S(1)}, s32[]{:S(2)}) async-start(s8[20971520]{0:T(1024)(128)(4,1)} %bitcast.4), calls=%async_computation.4 | async-start | bytes 8388608
  0.0 7.5 %collective-permute-start.5 = (bf16[32,640]{1,0:T(8,128)(2,1)}, bf16[32,640]{1,0:T(8,128)(2,1)S(1)}, u32[]{:S(2)}, u32[]{:S(2)}) collective-permute-start(bf16[32,640]{1,0:T(8,128)(2,1)} %bitcast.8), channel_id=1, source_target_pairs={{0,12},{2,14},{4,8},{6,10},{8,4},{10,6},{12,0},{14,2},{1,13},{3,15... | collective-permute-start | bytes 122888 | tf_op jit(solution)/shard_map/ppermute | solution.py:31
  5.2 5.1 %collective-permute-start.3 = (bf16[32,640]{1,0:T(8,128)(2,1)}, bf16[32,640]{1,0:T(8,128)(2,1)S(1)}, u32[]{:S(2)}, u32[]{:S(2)}) collective-permute-start(bf16[32,640]{1,0:T(8,128)(2,1)} %bitcast.9), channel_id=1, source_target_pairs={{0,8},{2,10},{4,12},{6,14},{8,0},{10,2},{12,4},{14,6},{1,9},{3,11}... | collective-permute-start | bytes 122888 | tf_op jit(solution)/shard_map/ppermute | solution.py:31
  5.2 6.6 %collective-permute-start.1 = (bf16[32,640]{1,0:T(8,128)(2,1)}, bf16[32,640]{1,0:T(8,128)(2,1)S(1)}, u32[]{:S(2)}, u32[]{:S(2)}) collective-permute-start(bf16[32,640]{1,0:T(8,128)(2,1)} %bitcast.10), channel_id=1, source_target_pairs={{0,4},{2,6},{4,0},{6,2},{8,12},{10,14},{12,8},{14,10},{1,5},{3,7},... | collective-permute-start | bytes 122888 | tf_op jit(solution)/shard_map/ppermute | solution.py:31
  5.8 6.5 %collective-permute-start = (bf16[32,640]{1,0:T(8,128)(2,1)}, bf16[32,640]{1,0:T(8,128)(2,1)S(1)}, u32[]{:S(2)}, u32[]{:S(2)}) collective-permute-start(bf16[32,640]{1,0:T(8,128)(2,1)} %bitcast.11), channel_id=1, source_target_pairs={{0,2},{2,0},{4,6},{6,4},{8,10},{10,8},{12,14},{14,12},{1,3},{3,1},... | collective-permute-start | bytes 122888 | tf_op jit(solution)/shard_map/ppermute | solution.py:31
  7.5 4.8 %collective-permute-start.6 = (bf16[32,640]{1,0:T(8,128)(2,1)S(1)}, bf16[32,640]{1,0:T(8,128)(2,1)S(1)}, u32[]{:S(2)}, u32[]{:S(2)}) collective-permute-start(bf16[32,640]{1,0:T(8,128)(2,1)S(1)} %shard_map.73.refs_7_), channel_id=1, source_target_pairs={{0,2},{2,0},{4,6},{6,4},{8,10},{10,8},{12,14},{14,12},{1,3},{3,1},... | collective-permute-start | bytes 122888 | tf_op jit(solution)/shard_map/ppermute | solution.py:31
  10.3 4.0 %collective-permute-start.4 = (bf16[32,640]{1,0:T(8,128)(2,1)S(1)}, bf16[32,640]{1,0:T(8,128)(2,1)S(1)}, u32[]{:S(2)}, u32[]{:S(2)}) collective-permute-start(bf16[32,640]{1,0:T(8,128)(2,1)S(1)} %collective-permute-done.3.refs_5_), channel_id=1, source_target_pairs={{0,2},{2,0},{4,6},{6,4},{8,10},{10,8},{12,14},{14,12},{1,3},{3,1},... | collective-permute-start | bytes 122888 | tf_op jit(solution)/shard_map/ppermute | solution.py:31
  11.8 4.0 %collective-permute-start.2 = (bf16[32,640]{1,0:T(8,128)(2,1)S(1)}, bf16[32,640]{1,0:T(8,128)(2,1)S(1)}, u32[]{:S(2)}, u32[]{:S(2)}) collective-permute-start(bf16[32,640]{1,0:T(8,128)(2,1)S(1)} %collective-permute-done.1.refs_3_), channel_id=1, source_target_pairs={{0,2},{2,0},{4,6},{6,4},{8,10},{10,8},{12,14},{14,12},{1,3},{3,1},... | collective-permute-start | bytes 122888 | tf_op jit(solution)/shard_map/ppermute | solution.py:31
  15.9 1.7 %copy-start = (bf16[10,40,512]{2,1,0:T(8,128)(2,1)S(1)}, bf16[10,40,512]{2,1,0:T(8,128)(2,1)}, u32[]{:S(2)}) copy-start(bf16[10,40,512]{2,1,0:T(8,128)(2,1)} %refs_3_.7) | copy-start | bytes 1228804
  15.9 1.7 %collective-permute-start.7 = (bf16[8,32,640]{2,1,0:T(8,128)(2,1)S(1)}, bf16[8,32,640]{2,1,0:T(8,128)(2,1)S(1)}, u32[]{:S(2)}, u32[]{:S(2)}) collective-permute-start(bf16[8,32,640]{2,1,0:T(8,128)(2,1)S(1)} %shard_map.74.refs_0_), channel_id=1, source_target_pairs={{0,1},{1,0},{2,3},{3,2},{4,5},{5,4},{6,7},{7,6},{8,9},{9,8},{10,11... | collective-permute-start | bytes 983048 | tf_op jit(solution)/shard_map/ppermute | solution.py:31
  19.4 5.5 %collective-permute-start.10 = (bf16[3,32,512]{2,1,0:T(8,128)(2,1)S(1)}, bf16[3,32,512]{2,1,0:T(8,128)(2,1)S(1)}, u32[]{:S(2)}, u32[]{:S(2)}) collective-permute-start(bf16[3,32,512]{2,1,0:T(8,128)(2,1)S(1)} %get-tuple-element.26), channel_id=1, source_target_pairs={{0,16},{16,0},{1,17},{17,1},{2,18},{18,2},{3,19},{19,3},{4,20},{20... | collective-permute-start | bytes 294920 | tf_op jit(solution)/shard_map/ppermute | solution.py:31
  21.8 3.0 %copy-start.1 = (f32[10,512]{1,0:T(8,128)S(1)}, f32[10,512]{1,0:T(8,128)}, u32[]{:S(2)}) copy-start(f32[10,512]{1,0:T(8,128)} %refs_4_.5) | copy-start | bytes 61444
  21.9 3.0 %copy-start.3 = (s32[10]{0:T(128)S(1)}, s32[10]{0:T(128)}, u32[]{:S(2)}) copy-start(s32[10]{0:T(128)} %refs_0_.7) | copy-start | bytes 124
  21.9 4.7 %collective-permute-start.9 = (bf16[2,32,512]{2,1,0:T(8,128)(2,1)S(1)}, bf16[2,32,512]{2,1,0:T(8,128)(2,1)S(1)}, u32[]{:S(2)}, u32[]{:S(2)}) collective-permute-start(bf16[2,32,512]{2,1,0:T(8,128)(2,1)S(1)} %get-tuple-element.23.refs_2_), channel_id=1, source_target_pairs={{0,16},{16,0},{1,17},{17,1},{2,18},{18,2},{3,19},{19,3},{4,20},{20... | collective-permute-start | bytes 196616 | tf_op jit(solution)/shard_map/ppermute | solution.py:31
  23.3 4.4 %collective-permute-start.8 = (f32[32,256]{1,0:T(8,128)S(1)}, f32[32,256]{1,0:T(8,128)S(1)}, u32[]{:S(2)}, u32[]{:S(2)}) collective-permute-start(f32[32,256]{1,0:T(8,128)S(1)} %shard_map.78.refs_6_.refs_0_), channel_id=1, source_target_pairs={{0,16},{16,0},{1,17},{17,1},{2,18},{18,2},{3,19},{19,3},{4,20},{20... | collective-permute-start | bytes 98312 | tf_op jit(solution)/shard_map/ppermute | solution.py:31
  28.2 1.5 %collective-permute-start.11 = (bf16[4,32,640]{2,1,0:T(8,128)(2,1)S(1)}, bf16[4,32,640]{2,1,0:T(8,128)(2,1)S(1)}, u32[]{:S(2)}, u32[]{:S(2)}) collective-permute-start(bf16[4,32,640]{2,1,0:T(8,128)(2,1)S(1)} %get-tuple-element.28), channel_id=1, source_target_pairs={{0,1},{1,0},{2,3},{3,2},{4,5},{5,4},{6,7},{7,6},{8,9},{9,8},{10,11... | collective-permute-start | bytes 491528 | tf_op jit(solution)/shard_map/ppermute | solution.py:31
  29.7 12.6 %copy-start.4 = (f32[640]{0:T(1024)S(1)}, f32[640]{0:T(1024)}, u32[]{:S(2)}) copy-start(f32[640]{0:T(1024)} %param.8) | copy-start | bytes 7684
  30.3 1.5 %collective-permute-start.15 = (bf16[4,32,640]{2,1,0:T(8,128)(2,1)S(1)}, bf16[4,32,640]{2,1,0:T(8,128)(2,1)S(1)}, u32[]{:S(2)}, u32[]{:S(2)}) collective-permute-start(bf16[4,32,640]{2,1,0:T(8,128)(2,1)S(1)} %get-tuple-element.34), channel_id=1, source_target_pairs={{0,1},{1,0},{2,3},{3,2},{4,5},{5,4},{6,7},{7,6},{8,9},{9,8},{10,11... | collective-permute-start | bytes 491528 | tf_op jit(solution)/shard_map/ppermute | solution.py:31
  30.5 5.2 %collective-permute-start.12 = (bf16[2,32,640]{2,1,0:T(8,128)(2,1)S(1)}, bf16[2,32,640]{2,1,0:T(8,128)(2,1)S(1)}, u32[]{:S(2)}, u32[]{:S(2)}) collective-permute-start(bf16[2,32,640]{2,1,0:T(8,128)(2,1)S(1)} %get-tuple-element.30), channel_id=1, source_target_pairs={{0,2},{2,0},{4,6},{6,4},{8,10},{10,8},{12,14},{14,12},{1,3},{3,1},... | collective-permute-start | bytes 245768 | tf_op jit(solution)/shard_map/ppermute | solution.py:31
  31.8 6.0 %collective-permute-start.16 = (bf16[2,32,640]{2,1,0:T(8,128)(2,1)S(1)}, bf16[2,32,640]{2,1,0:T(8,128)(2,1)S(1)}, u32[]{:S(2)}, u32[]{:S(2)}) collective-permute-start(bf16[2,32,640]{2,1,0:T(8,128)(2,1)S(1)} %get-tuple-element.36), channel_id=1, source_target_pairs={{0,2},{2,0},{4,6},{6,4},{8,10},{10,8},{12,14},{14,12},{1,3},{3,1},... | collective-permute-start | bytes 245768 | tf_op jit(solution)/shard_map/ppermute | solution.py:31
  35.8 5.0 %collective-permute-start.13 = (bf16[32,640]{1,0:T(8,128)(2,1)S(1)}, bf16[32,640]{1,0:T(8,128)(2,1)S(1)}, u32[]{:S(2)}, u32[]{:S(2)}) collective-permute-start(bf16[32,640]{1,0:T(8,128)(2,1)S(1)} %get-tuple-element.31), channel_id=1, source_target_pairs={{0,8},{2,10},{4,12},{6,14},{8,0},{10,2},{12,4},{14,6},{1,9},{3,11}... | collective-permute-start | bytes 122888 | tf_op jit(solution)/shard_map/ppermute | solution.py:31
  36.4 5.9 %collective-permute-start.14 = (bf16[32,640]{1,0:T(8,128)(2,1)S(1)}, bf16[32,640]{1,0:T(8,128)(2,1)S(1)}, u32[]{:S(2)}, u32[]{:S(2)}) collective-permute-start(bf16[32,640]{1,0:T(8,128)(2,1)S(1)} %get-tuple-element.32), channel_id=1, source_target_pairs={{0,12},{2,14},{4,8},{6,10},{8,4},{10,6},{12,0},{14,2},{1,13},{3,15... | collective-permute-start | bytes 122888 | tf_op jit(solution)/shard_map/ppermute | solution.py:31
  37.8 4.5 %collective-permute-start.17 = (bf16[32,640]{1,0:T(8,128)(2,1)S(1)}, bf16[32,640]{1,0:T(8,128)(2,1)S(1)}, u32[]{:S(2)}, u32[]{:S(2)}) collective-permute-start(bf16[32,640]{1,0:T(8,128)(2,1)S(1)} %get-tuple-element.38), channel_id=1, source_target_pairs={{0,4},{2,6},{4,0},{6,2},{8,12},{10,14},{12,8},{14,10},{1,5},{3,7},... | collective-permute-start | bytes 122888 | tf_op jit(solution)/shard_map/ppermute | solution.py:31

commit v3 on v2

--- a/solution.py
+++ b/solution.py
@@ -159,28 +159,35 @@
     refs[-1][...] = value
 
 
-def grid_kernel(plan, part, span, skip, live, dens_a, dens_b, occ, weight, vir, *refs):
+def grid_kernel(plan, part, spans, more, live, *refs):
+    pairs = refs[: 2 * len(spans)]
+    occ, weight, vir = refs[2 * len(spans) : 2 * len(spans) + 3]
     acc, scaled, occ32 = refs[-3:]
     k = plan.k
     base = lax.axis_index("vec") * plan.batches
     slots = lax.broadcasted_iota(jnp.int32, (1, plan.points), 1)
-    for n, b in enumerate(span):
-        row = occ_rows(plan, occ, b, occ32.at[n])
-        density = dens_a[n] + dens_b[n].astype(jnp.float32)
-        used = jnp.where(slots < live[base + b], weight[pl.ds(base + b, 1), :], 0.0)
-        weighted = density * used
-        for t, d in enumerate(part):
-            first = plan.first_row(d)
-            for r in range(plan.run):
-                at = (t * plan.run + r) * k
-                scaled[at : at + k, :] = (row(first + r) * weighted).astype(jnp.bfloat16)
-        value = lax.dot_general(scaled[...], vir[base + b], NN, preferred_element_type=jnp.float32)
-        if n:
-            acc[...] += value
-        elif skip is None:
-            acc[...] = value
-        else:
-            acc[...] = refs[0][pl.ds(skip, acc.shape[0]), :] + value
+    begun = more
+    for c, span in enumerate(spans):
+        for n, b in enumerate(span):
+            row = occ_rows(plan, occ, b, occ32.at[b - spans[0][0]])
+            density = pairs[2 * c][n] + pairs[2 * c + 1][n].astype(jnp.float32)
+            used = jnp.where(slots < live[base + b], weight[pl.ds(base + b, 1), :], 0.0)
+            weighted = density * used
+            for t, d in enumerate(part):
+                first = plan.first_row(d)
+                for r in range(plan.run):
+                    at = (t * plan.run + r) * k
+                    scaled[at : at + k, :] = (row(first + r) * weighted).astype(jnp.bfloat16)
+            value = lax.dot_general(
+                scaled[...], vir[base + b], NN, preferred_element_type=jnp.float32
+            )
+            if not begun:
+                acc[...] = value
+            elif more and c == n == 0:
+                acc[...] = refs[2 * len(spans) + 3][...] + value
+            else:
+                acc[...] += value
+            begun = True
 
 
 def back_kernel(plan, part, part_a, part_b, fac, acc, stay, sent):
@@ -238,7 +245,7 @@
     pieces, masks = [trial_cols], [0]
     for stride, radix in reversed(digits):
         known = len(masks)
-        for d in range(1, radix):
+        for d in range(radix - 1, 0, -1):
             for n in range(known):
                 pieces.append(swap(pieces[n], "blk", blks, d * stride))
                 masks.append(masks[n] ^ (d * stride))
@@ -295,24 +302,25 @@
     )(other, coulomb_factors, sent, part)
     other_part = swap(part, "grp", groups, 1)
 
-    def grid(chosen, chunk, dens, came, skip, *more):
+    density = [(first_dens, first_other), (second_dens, second_other)]
+
+    def grid(number, chunks, begun=(), order=()):
+        chosen = plan.parts[number]
         used = plan.run * len(chosen)
-        count = 6 + (skip is not None)
-        body = bind(grid_kernel, chosen, spans[chunk], skip)
+        body = bind(grid_kernel, chosen, [spans[c] for c in chunks], len(begun) > 0)
+        given = [x for c in chunks for x in density[c]]
+        count = 4 + len(given) + len(begun)
+        batch = sum(spans[c][-1] + 1 - spans[c][0] for c in chunks)
         return call(
-            after(body, count) if len(more) + 6 > count else body,
+            after(body, count) if order else body,
             shape((used * k, virs), f32),
-            [SMEM] + [VMEM] * (count - 1) + [ANY] * (len(more) + 6 - count),
-            grid_flops * len(spans[chunk]) * used // occs,
-            [pltpu.VMEM((used * k, points), bf16), occ_scratch(spans[chunk])],
-        )(live_points, dens, came, occ_values, kernel, vir_values, *more)
-
-    every = sum(plan.parts, ())
-    begun = grid(every, 0, first_dens, first_other, None, part)
-
-    def finish(number, *order):
-        skip = sum(len(chosen) for chosen in plan.parts[:number]) * plan.run * k
-        return grid(plan.parts[number], 1, second_dens, second_other, skip, begun, *order)
+            [SMEM] + [VMEM] * (count - 1) + [ANY] * len(order),
+            grid_flops * batch * used // occs,
+            [
+                pltpu.VMEM((used * k, points), bf16),
+                pltpu.VMEM((batch, plan.occ_all, points), f32),
+            ],
+        )(live_points, *given, occ_values, kernel, vir_values, *begun, *order)
 
     def back(number, acc, *order):
         chosen = plan.parts[number]
@@ -347,14 +355,14 @@
                 for d, x in zip(plan.parts[number], outs)
             ]
 
-        stay, sent = back(0, finish(0))
-        acc = finish(1, stay)
+        stay, sent = back(0, grid(0, (1,), (grid(0, (0,), (), (part,)),)))
+        acc = grid(1, (0, 1), (), (stay,))
         far = first_sum(stay, sent, acc)
         stay, sent = back(1, acc, far[0])
         near = first_sum(stay, sent)
         came = next_sum(0, far[0], far[1:]) + next_sum(1, near[0], near[1:])
     else:
-        stay, sent = back(0, finish(0))
+        stay, sent = back(0, grid(0, (0, 1)))
         full = jnp.concatenate([stay[0], sent[0].astype(f32)], axis=1)
         full = full.reshape(k, blks, vecs, plan.rows).transpose(2, 1, 0, 3)
         full = jnp.take(full, me ^ jnp.arange(blks), axis=1)

time: 43.1 us -> 43.1 us (level)
  starting transfers between devices: 20.4 us -> 21.5 us
  waiting for transfers between devices: 12.2 us -> 11.1 us
    ppermute x18, waiting for transfers between devices: 12.2 us -> 11.1 us  [swap(): return lax.ppermute(x, axis, [(i, i ^ mask) for i in range(count)])]
    ppermute x18, starting transfers between devices: 20.4 us -> 21.5 us  [swap(): return lax.ppermute(x, axis, [(i, i ^ mask) for i in range(count)])]
where the time goes in v3:
time: 43.1 us; the launch traced here: 42.9 us
  starting transfers between devices  21.5 us (50%)
  waiting for transfers between devices  11.1 us (26%)
  Pallas kernels  9.38 us (22%)
  other arithmetic  0.65 us (2%)
    ppermute x18, starting transfers between devices, swap(): return lax.ppermute(x, axis, [(i, i ^ mask) for i in range(count)])  21.5 us
    ppermute x18, waiting for transfers between devices, swap(): return lax.ppermute(x, axis, [(i, i ^ mask) for i in range(count)])  11.1 us
    pallas_call x3, Pallas kernels, grid(): call(after(body, count) if order else body, shape((used * k, virs), f32),...  3.82 us
    pallas_call x1, Pallas kernels, local(): call(after(bind(first_dens_kernel, spans[0]), 4), (shape(chunks[0], f32),...  1.76 us
    pallas_call x2, Pallas kernels, back(): call(after(body, 4) if order else body, (shape(share, f32), shape(share,...  1.07 us
    pallas_call x1, Pallas kernels, local(): call(bind(dens_kernel, spans[1]), (shape(chunks[1], f32), shape(chunks[1]...  0.88 us
    pallas_call x1, Pallas kernels, local(): call(bind(fac_kernel, 0), shape((k, plan.aux), f32), [VMEM] * 2, flops)  0.87 us
  transfers between devices with their start and end apart: 18, of which 9 were waited for; matrix products, arithmetic and copies ran while one was open for 0% of the time, Pallas kernels for 15%

profile of v3, /device:TPU:0, one launch (start us, length us, event | category | flops | bytes accessed | tf_op | source)
XLA Modules:
  0.0 42.9 jit_solution(15634801051821143495)
XLA Ops:
  0.0 0.0 slice-start.2
  0.0 0.0 slice-start.3
  0.0 0.0 slice-start.4
  0.0 3.1 %collective-permute-start.1 = (bf16[32,640]{1,0:T(8,128)(2,1)}, bf16[32,640]{1,0:T(8,128)(2,1)S(1)}, u32[]{:S(2)}, u32[]{:S(2)}) collective-permute-start(bf16[32,640]{1,0:T(8,128)(2,1)} %bitcast.8), channel_id=1, source_target_pairs={{0,4},{2,6},{4,0},{6,2},{8,12},{10,14},{12,8},{14,10},{1,5},{3,7},... | collective-permute-start | bytes 122888 | tf_op jit(solution)/shard_map/ppermute | solution.py:31
  3.2 2.6 %collective-permute-start.3 = (bf16[32,640]{1,0:T(8,128)(2,1)}, bf16[32,640]{1,0:T(8,128)(2,1)S(1)}, u32[]{:S(2)}, u32[]{:S(2)}) collective-permute-start(bf16[32,640]{1,0:T(8,128)(2,1)} %bitcast.9), channel_id=1, source_target_pairs={{0,8},{2,10},{4,12},{6,14},{8,0},{10,2},{12,4},{14,6},{1,9},{3,11}... | collective-permute-start | bytes 122888 | tf_op jit(solution)/shard_map/ppermute | solution.py:31
  5.8 0.0 collective-permute-start.5
  5.8 1.7 %collective-permute-start = (bf16[32,640]{1,0:T(8,128)(2,1)}, bf16[32,640]{1,0:T(8,128)(2,1)S(1)}, u32[]{:S(2)}, u32[]{:S(2)}) collective-permute-start(bf16[32,640]{1,0:T(8,128)(2,1)} %bitcast.11), channel_id=1, source_target_pairs={{0,2},{2,0},{4,6},{6,4},{8,10},{10,8},{12,14},{14,12},{1,3},{3,1},... | collective-permute-start | bytes 122888 | tf_op jit(solution)/shard_map/ppermute | solution.py:31
  7.5 0.0 collective-permute-done.1.refs_0_
  7.5 0.4 collective-permute-start.2
  7.9 1.2 %collective-permute-done.3.refs_5_ = bf16[32,640]{1,0:T(8,128)(2,1)S(1)} collective-permute-done((bf16[32,640]{1,0:T(8,128)(2,1)}, bf16[32,640]{1,0:T(8,128)(2,1)S(1)}, u32[]{:S(2)}, u32[]{:S(2)}) %collective-permute-start.3) | collective-permute-done | bytes 40992 | tf_op jit(solution)/shard_map/ppermute | solution.py:31
  9.1 1.5 %collective-permute-start.4 = (bf16[32,640]{1,0:T(8,128)(2,1)S(1)}, bf16[32,640]{1,0:T(8,128)(2,1)S(1)}, u32[]{:S(2)}, u32[]{:S(2)}) collective-permute-start(bf16[32,640]{1,0:T(8,128)(2,1)S(1)} %collective-permute-done.3.refs_5_), channel_id=1, source_target_pairs={{0,2},{2,0},{4,6},{6,4},{8,10},{10,8},{12,14},{14,12},{1,3},{3,1},... | collective-permute-start | bytes 122888 | tf_op jit(solution)/shard_map/ppermute | solution.py:31
  10.6 1.2 %collective-permute-done.5.refs_7_ = bf16[32,640]{1,0:T(8,128)(2,1)S(1)} collective-permute-done((bf16[32,640]{1,0:T(8,128)(2,1)}, bf16[32,640]{1,0:T(8,128)(2,1)S(1)}, u32[]{:S(2)}, u32[]{:S(2)}) %collective-permute-start.5) | collective-permute-done | bytes 40992 | tf_op jit(solution)/shard_map/ppermute | solution.py:31
  11.8 1.5 %collective-permute-start.6 = (bf16[32,640]{1,0:T(8,128)(2,1)S(1)}, bf16[32,640]{1,0:T(8,128)(2,1)S(1)}, u32[]{:S(2)}, u32[]{:S(2)}) collective-permute-start(bf16[32,640]{1,0:T(8,128)(2,1)S(1)} %collective-permute-done.5.refs_7_), channel_id=1, source_target_pairs={{0,2},{2,0},{4,6},{6,4},{8,10},{10,8},{12,14},{14,12},{1,3},{3,1},... | collective-permute-start | bytes 122888 | tf_op jit(solution)/shard_map/ppermute | solution.py:31
  13.3 0.0 collective-permute-done.refs_2_
  13.3 0.0 collective-permute-done.2.refs_4_
  13.3 0.2 collective-permute-done.4.refs_6_
  13.5 2.3 %collective-permute-done.6.refs_8_ = bf16[32,640]{1,0:T(8,128)(2,1)S(1)} collective-permute-done((bf16[32,640]{1,0:T(8,128)(2,1)S(1)}, bf16[32,640]{1,0:T(8,128)(2,1)S(1)}, u32[]{:S(2)}, u32[]{:S(2)}) %collective-permute-start.6) | collective-permute-done | bytes 40992 | tf_op jit(solution)/shard_map/ppermute | solution.py:31
  15.8 0.0 copy-done.2
  15.8 0.0 slice-done.5
  15.8 0.0 slice-done.6
  15.8 0.1 collective-permute-start.7
  15.9 0.0 slice-done
  15.9 0.0 slice-done.1
  15.9 0.0 slice-done.2
  15.9 0.0 slice-done.3
  16.0 0.0 slice-done.4
  16.0 0.9 %shard_map.75.refs_4_.refs_3_ = f32[32,256]{1,0:T(8,128)S(1)} custom-call(bf16[8,32,640]{2,1,0:T(8,128)(2,1)S(1)} %shard_map.74.refs_0_, bf16[512,20480]{1,0:T(8,128)(2,1)S(1)} %bitcast.5), custom_call_target="tpu_custom_call" | custom-call | flops 83886080 | tf_op jit(solution)/shard_map/pallas_call | solution.py:272
  16.8 0.0 copy-start.1
  16.9 0.0 copy-start.3
  16.9 0.7 %collective-permute-done.7.refs_1_.refs_0_ = bf16[8,32,640]{2,1,0:T(8,128)(2,1)S(1)} collective-permute-done((bf16[8,32,640]{2,1,0:T(8,128)(2,1)S(1)}, bf16[8,32,640]{2,1,0:T(8,128)(2,1)S(1)}, u32[]{:S(2)}, u32[]{:S(2)}) %collective-permute-start.7) | collective-permute-done | bytes 327712 | tf_op jit(solution)/shard_map/ppermute | solution.py:31
  17.5 0.0 copy-done
  17.5 1.8 %shard_map.76 = (f32[3,32,512]{2,1,0:T(8,128)S(1)}, bf16[3,32,512]{2,1,0:T(8,128)(2,1)S(1)}, bf16[640,512]{1,0:T(8,128)(2,1)S(1)}) custom-call(bf16[8,32,640]{2,1,0:T(8,128)(2,1)S(1)} %shard_map.74.refs_0_, bf16[8,32,640]{2,1,0:T(8,128)(2,1)S(1)} %collective-permute-done.7.refs_1_.refs_0_, bf16[10,512,512]{2,1,0:T(8,128)(2,1)S(1)} %bitcast.7, ...), custom_call_target="tpu_custom_call" | custom-call | flops 1006632960 | tf_op jit(solution)/shard_map/pallas_call | solution.py:284
  19.3 1.6 %collective-permute-start.10 = (bf16[3,32,512]{2,1,0:T(8,128)(2,1)S(1)}, bf16[3,32,512]{2,1,0:T(8,128)(2,1)S(1)}, u32[]{:S(2)}, u32[]{:S(2)}) collective-permute-start(bf16[3,32,512]{2,1,0:T(8,128)(2,1)S(1)} %get-tuple-element.26), channel_id=1, source_target_pairs={{0,16},{16,0},{1,17},{17,1},{2,18},{18,2},{3,19},{19,3},{4,20},{20... | collective-permute-start | bytes 294920 | tf_op jit(solution)/shard_map/ppermute | solution.py:31
  20.9 0.9 %shard_map.77 = (f32[2,32,512]{2,1,0:T(8,128)S(1)}, bf16[2,32,512]{2,1,0:T(8,128)(2,1)S(1)}) custom-call(bf16[640,512]{1,0:T(8,128)(2,1)S(1)} %get-tuple-element.22.refs_0_, bf16[10,512,512]{2,1,0:T(8,128)(2,1)S(1)} %bitcast.7, bf16[10,40,512]{2,1,0:T(8,128)(2,1)S(1)} %copy-done), custom_call_target="tpu_custom_call" | custom-call | flops 671088640 | tf_op jit(solution)/shard_map/pallas_call | solution.py:292
  21.7 0.6 %collective-permute-start.9 = (bf16[2,32,512]{2,1,0:T(8,128)(2,1)S(1)}, bf16[2,32,512]{2,1,0:T(8,128)(2,1)S(1)}, u32[]{:S(2)}, u32[]{:S(2)}) collective-permute-start(bf16[2,32,512]{2,1,0:T(8,128)(2,1)S(1)} %get-tuple-element.23.refs_2_), channel_id=1, source_target_pairs={{0,16},{16,0},{1,17},{17,1},{2,18},{18,2},{3,19},{19,3},{4,20},{20... | collective-permute-start | bytes 196616 | tf_op jit(solution)/shard_map/ppermute | solution.py:31
  22.4 0.8 %shard_map.78.refs_6_.refs_0_ = f32[32,256]{1,0:T(8,128)S(1)} custom-call(bf16[8,32,640]{2,1,0:T(8,128)(2,1)S(1)} %collective-permute-done.7.refs_1_.refs_0_, bf16[512,20480]{1,0:T(8,128)(2,1)S(1)} %bitcast.5, bf16[2,32,512]{2,1,0:T(8,128)(2,1)S(1)} %get-tuple-element.23.refs_2_, f32[32,256]{1,0:T(8,128)S(1)} %shard_map.75.refs_4_.refs_3_), custom_call_target="tpu_custom_call" | custom-call | flops 83886080 | tf_op jit(solution)/shard_map/pallas_call | solution.py:300
  23.2 1.5 %collective-permute-start.8 = (f32[32,256]{1,0:T(8,128)S(1)}, f32[32,256]{1,0:T(8,128)S(1)}, u32[]{:S(2)}, u32[]{:S(2)}) collective-permute-start(f32[32,256]{1,0:T(8,128)S(1)} %shard_map.78.refs_6_.refs_0_), channel_id=1, source_target_pairs={{0,16},{16,0},{1,17},{17,1},{2,18},{18,2},{3,19},{19,3},{4,20},{20... | collective-permute-start | bytes 98312 | tf_op jit(solution)/shard_map/ppermute | solution.py:31
  24.7 0.0 collective-permute-done.10.refs_2_
  24.7 0.0 copy-done.1
  24.7 0.0 copy-done.3
  24.8 1.2 %shard_map.79.refs_6_ = f32[320,512]{1,0:T(8,128)S(1)} custom-call(s32[10]{0:T(128)S(1)} %copy-done.3, f32[3,32,512]{2,1,0:T(8,128)S(1)} %get-tuple-element.25.refs_1_, bf16[3,32,512]{2,1,0:T(8,128)(2,1)S(1)} %collective-permute-done.10.refs_2_, bf16[10,40,512]{2,1,0:T(8,128)(2,1)S(1)} %copy-done, f32[10,512]{1,0:T(8,128)S(1)} %copy-done.1, ...), custom_call_target="tpu_custom_call" | custom-call | flops 503316480 | tf_op jit(solution)/shard_map/pallas_call | solution.py:314
  26.0 0.5 %collective-permute-done.9.refs_2_.refs_4_ = bf16[2,32,512]{2,1,0:T(8,128)(2,1)S(1)} collective-permute-done((bf16[2,32,512]{2,1,0:T(8,128)(2,1)S(1)}, bf16[2,32,512]{2,1,0:T(8,128)(2,1)S(1)}, u32[]{:S(2)}, u32[]{:S(2)}) %collective-permute-start.9) | collective-permute-done | bytes 65568 | tf_op jit(solution)/shard_map/ppermute | solution.py:31
  26.4 1.0 %shard_map.80.refs_3_ = f32[320,512]{1,0:T(8,128)S(1)} custom-call(s32[10]{0:T(128)S(1)} %copy-done.3, f32[2,32,512]{2,1,0:T(8,128)S(1)} %get-tuple-element.24.refs_1_.refs_3_, bf16[2,32,512]{2,1,0:T(8,128)(2,1)S(1)} %collective-permute-done.9.refs_2_.refs_4_, bf16[10,40,512]{2,1,0:T(8,128)(2,1)S(1)} %copy-done, f32[10,512]{1,0:T(8,128)S(1)} %copy-done.1, ...), custom_call_target="tpu_custom_call" | custom-call | flops 335544320 | tf_op jit(solution)/shard_map/pallas_call | solution.py:314
  27.5 0.0 collective-permute-done.8.refs_1_
  27.5 0.5 %shard_map.81 = (f32[4,32,640]{2,1,0:T(8,128)S(1)}, bf16[4,32,640]{2,1,0:T(8,128)(2,1)S(1)}) custom-call(f32[32,256]{1,0:T(8,128)S(1)} %shard_map.78.refs_6_.refs_0_, f32[32,256]{1,0:T(8,128)S(1)} %collective-permute-done.8.refs_1_, bf16[512,20480]{1,0:T(8,128)(2,1)S(1)} %bitcast.5, f32[320,512]{1,0:T(8,128)S(1)} %shard_map.80.refs_3_), custom_call_target="tpu_custom_call" | custom-call | flops 83886080 | tf_op jit(solution)/shard_map/pallas_call | solution.py:329
  28.0 0.0 copy-start.4
  28.1 0.1 collective-permute-start.11
  28.1 1.6 %shard_map.82.refs_2_.refs_3_ = f32[320,512]{1,0:T(8,128)S(1)} custom-call(s32[10]{0:T(128)S(1)} %copy-done.3, f32[3,32,512]{2,1,0:T(8,128)S(1)} %get-tuple-element.25.refs_1_, bf16[3,32,512]{2,1,0:T(8,128)(2,1)S(1)} %collective-permute-done.10.refs_2_, f32[2,32,512]{2,1,0:T(8,128)S(1)} %get-tuple-element.24.refs_1_.refs_3_, ...), custom_call_target="tpu_custom_call" | custom-call | flops 838860800 | tf_op jit(solution)/shard_map/pallas_call | solution.py:314
  29.7 0.0 collective-permute-done.11.refs_1_
  29.7 0.5 %shard_map.85 = (f32[4,32,640]{2,1,0:T(8,128)S(1)}, bf16[4,32,640]{2,1,0:T(8,128)(2,1)S(1)}) custom-call(f32[32,256]{1,0:T(8,128)S(1)} %shard_map.78.refs_6_.refs_0_, f32[32,256]{1,0:T(8,128)S(1)} %collective-permute-done.8.refs_1_, bf16[512,20480]{1,0:T(8,128)(2,1)S(1)} %bitcast.5, f32[320,512]{1,0:T(8,128)S(1)} %shard_map.82.refs_2_.refs_3_, ...), custom_call_target="tpu_custom_call" | custom-call | flops 83886080 | tf_op jit(solution)/shard_map/pallas_call | solution.py:329
  30.3 0.6 %collective-permute-start.15 = (bf16[4,32,640]{2,1,0:T(8,128)(2,1)S(1)}, bf16[4,32,640]{2,1,0:T(8,128)(2,1)S(1)}, u32[]{:S(2)}, u32[]{:S(2)}) collective-permute-start(bf16[4,32,640]{2,1,0:T(8,128)(2,1)S(1)} %get-tuple-element.34), channel_id=1, source_target_pairs={{0,1},{1,0},{2,3},{3,2},{4,5},{5,4},{6,7},{7,6},{8,9},{9,8},{10,11... | collective-permute-start | bytes 491528 | tf_op jit(solution)/shard_map/ppermute | solution.py:31
  30.9 1.5 %collective-permute-start.12 = (bf16[2,32,640]{2,1,0:T(8,128)(2,1)S(1)}, bf16[2,32,640]{2,1,0:T(8,128)(2,1)S(1)}, u32[]{:S(2)}, u32[]{:S(2)}) collective-permute-start(bf16[2,32,640]{2,1,0:T(8,128)(2,1)S(1)} %get-tuple-element.30), channel_id=1, source_target_pairs={{0,2},{2,0},{4,6},{6,4},{8,10},{10,8},{12,14},{14,12},{1,3},{3,1},... | collective-permute-start | bytes 245768 | tf_op jit(solution)/shard_map/ppermute | solution.py:31
  32.4 0.0 collective-permute-done.15.refs_1_
  32.4 1.1 %collective-permute-start.16 = (bf16[2,32,640]{2,1,0:T(8,128)(2,1)S(1)}, bf16[2,32,640]{2,1,0:T(8,128)(2,1)S(1)}, u32[]{:S(2)}, u32[]{:S(2)}) collective-permute-start(bf16[2,32,640]{2,1,0:T(8,128)(2,1)S(1)} %get-tuple-element.36), channel_id=1, source_target_pairs={{0,2},{2,0},{4,6},{6,4},{8,10},{10,8},{12,14},{14,12},{1,3},{3,1},... | collective-permute-start | bytes 245768 | tf_op jit(solution)/shard_map/ppermute | solution.py:31
  33.5 2.1 %collective-permute-done.12.refs_1_ = bf16[2,32,640]{2,1,0:T(8,128)(2,1)S(1)} collective-permute-done((bf16[2,32,640]{2,1,0:T(8,128)(2,1)S(1)}, bf16[2,32,640]{2,1,0:T(8,128)(2,1)S(1)}, u32[]{:S(2)}, u32[]{:S(2)}) %collective-permute-start.12) | collective-permute-done | bytes 81952 | tf_op jit(solution)/shard_map/ppermute | solution.py:31
  35.7 0.8 %collective-permute-start.13 = (bf16[32,640]{1,0:T(8,128)(2,1)S(1)}, bf16[32,640]{1,0:T(8,128)(2,1)S(1)}, u32[]{:S(2)}, u32[]{:S(2)}) collective-permute-start(bf16[32,640]{1,0:T(8,128)(2,1)S(1)} %get-tuple-element.31), channel_id=1, source_target_pairs={{0,8},{2,10},{4,12},{6,14},{8,0},{10,2},{12,4},{14,6},{1,9},{3,11}... | collective-permute-start | bytes 122888 | tf_op jit(solution)/shard_map/ppermute | solution.py:31
  36.5 0.8 %collective-permute-start.14 = (bf16[32,640]{1,0:T(8,128)(2,1)S(1)}, bf16[32,640]{1,0:T(8,128)(2,1)S(1)}, u32[]{:S(2)}, u32[]{:S(2)}) collective-permute-start(bf16[32,640]{1,0:T(8,128)(2,1)S(1)} %get-tuple-element.32), channel_id=1, source_target_pairs={{0,12},{2,14},{4,8},{6,10},{8,4},{10,6},{12,0},{14,2},{1,13},{3,15... | collective-permute-start | bytes 122888 | tf_op jit(solution)/shard_map/ppermute | solution.py:31
  37.3 0.0 collective-permute-done.16.refs_1_
  37.3 2.0 %collective-permute-start.17 = (bf16[32,640]{1,0:T(8,128)(2,1)S(1)}, bf16[32,640]{1,0:T(8,128)(2,1)S(1)}, u32[]{:S(2)}, u32[]{:S(2)}) collective-permute-start(bf16[32,640]{1,0:T(8,128)(2,1)S(1)} %get-tuple-element.38), channel_id=1, source_target_pairs={{0,4},{2,6},{4,0},{6,2},{8,12},{10,14},{12,8},{14,10},{1,5},{3,7},... | collective-permute-start | bytes 122888 | tf_op jit(solution)/shard_map/ppermute | solution.py:31
  39.3 1.3 %collective-permute-done.13 = bf16[32,640]{1,0:T(8,128)(2,1)S(1)} collective-permute-done((bf16[32,640]{1,0:T(8,128)(2,1)S(1)}, bf16[32,640]{1,0:T(8,128)(2,1)S(1)}, u32[]{:S(2)}, u32[]{:S(2)}) %collective-permute-start.13) | collective-permute-done | bytes 40992 | tf_op jit(solution)/shard_map/ppermute | solution.py:31
  40.6 1.6 %collective-permute-done.14 = bf16[32,640]{1,0:T(8,128)(2,1)S(1)} collective-permute-done((bf16[32,640]{1,0:T(8,128)(2,1)S(1)}, bf16[32,640]{1,0:T(8,128)(2,1)S(1)}, u32[]{:S(2)}, u32[]{:S(2)}) %collective-permute-start.14) | collective-permute-done | bytes 40992 | tf_op jit(solution)/shard_map/ppermute | solution.py:31
  42.3 0.0 collective-permute-done.17
  42.3 0.0 copy-done.4
  42.3 0.7 %fusion = bf16[640,32]{0,1:T(8,128)(2,1)} fusion(bf16[32,640]{1,0:T(8,128)(2,1)S(1)} %collective-permute-done.17, f32[32,640]{1,0:T(8,128)S(1)} %get-tuple-element.37, bf16[32,640]{1,0:T(8,128)(2,1)S(1)} %collective-permute-done.14, bf16[32,640]{1,0:T(8,128)(2,1)S(1)} %collective-permute-done.13, f32[640]{0:T(1024)S(1)} %copy-done.4, ...), kind=kLoop, calls=%fused_computation.1 | loop fusion | flops 204800 | bytes 289280 | tf_op jit(solution)/shard_map/transpose | solution.py:383
  (14 shorter events, 0.1 us)
Async XLA Ops:
  0.0 15.8 %copy-start.2 = (bf16[640,32]{0,1:T(8,128)(2,1)S(1)}, bf16[640,32]{0,1:T(8,128)(2,1)}, u32[]{:S(2)}) copy-start(bf16[640,32]{0,1:T(8,128)(2,1)} %param.7) | copy-start | bytes 122884
  0.0 15.8 %slice-start.5 = ((s8[5242880]{0:T(1024)(128)(4,1)}), s8[4194304]{0:T(1024)(128)(4,1)S(1)}, s32[]{:S(2)}) async-start(s8[5242880]{0:T(1024)(128)(4,1)} %bitcast.6), calls=%async_computation.5 | async-start | bytes 8388608
  0.0 15.9 %slice-start = ((s8[20971520]{0:T(1024)(128)(4,1)}), s8[4194304]{0:T(1024)(128)(4,1)S(1)}, s32[]{:S(2)}) async-start(s8[20971520]{0:T(1024)(128)(4,1)} %bitcast.4), calls=%async_computation | async-start | bytes 8388608
  0.0 15.8 %slice-start.6 = ((s8[5242880]{0:T(1024)(128)(4,1)}), s8[1048576]{0:T(1024)(128)(4,1)S(1)}, s32[]{:S(2)}) async-start(s8[5242880]{0:T(1024)(128)(4,1)} %bitcast.6), calls=%async_computation.6 | async-start | bytes 2097152
  0.0 15.9 %slice-start.1 = ((s8[20971520]{0:T(1024)(128)(4,1)}), s8[4194304]{0:T(1024)(128)(4,1)S(1)}, s32[]{:S(2)}) async-start(s8[20971520]{0:T(1024)(128)(4,1)} %bitcast.4), calls=%async_computation.1 | async-start | bytes 8388608
  0.0 15.9 %slice-start.2 = ((s8[20971520]{0:T(1024)(128)(4,1)}), s8[4194304]{0:T(1024)(128)(4,1)S(1)}, s32[]{:S(2)}) async-start(s8[20971520]{0:T(1024)(128)(4,1)} %bitcast.4), calls=%async_computation.2 | async-start | bytes 8388608
  0.0 15.9 %slice-start.3 = ((s8[20971520]{0:T(1024)(128)(4,1)}), s8[4194304]{0:T(1024)(128)(4,1)S(1)}, s32[]{:S(2)}) async-start(s8[20971520]{0:T(1024)(128)(4,1)} %bitcast.4), calls=%async_computation.3 | async-start | bytes 8388608
  0.0 15.9 %slice-start.4 = ((s8[20971520]{0:T(1024)(128)(4,1)}), s8[4194304]{0:T(1024)(128)(4,1)S(1)}, s32[]{:S(2)}) async-start(s8[20971520]{0:T(1024)(128)(4,1)} %bitcast.4), calls=%async_computation.4 | async-start | bytes 8388608
  0.0 7.5 %collective-permute-start.1 = (bf16[32,640]{1,0:T(8,128)(2,1)}, bf16[32,640]{1,0:T(8,128)(2,1)S(1)}, u32[]{:S(2)}, u32[]{:S(2)}) collective-permute-start(bf16[32,640]{1,0:T(8,128)(2,1)} %bitcast.8), channel_id=1, source_target_pairs={{0,4},{2,6},{4,0},{6,2},{8,12},{10,14},{12,8},{14,10},{1,5},{3,7},... | collective-permute-start | bytes 122888 | tf_op jit(solution)/shard_map/ppermute | solution.py:31
  3.2 5.9 %collective-permute-start.3 = (bf16[32,640]{1,0:T(8,128)(2,1)}, bf16[32,640]{1,0:T(8,128)(2,1)S(1)}, u32[]{:S(2)}, u32[]{:S(2)}) collective-permute-start(bf16[32,640]{1,0:T(8,128)(2,1)} %bitcast.9), channel_id=1, source_target_pairs={{0,8},{2,10},{4,12},{6,14},{8,0},{10,2},{12,4},{14,6},{1,9},{3,11}... | collective-permute-start | bytes 122888 | tf_op jit(solution)/shard_map/ppermute | solution.py:31
  5.8 6.0 %collective-permute-start.5 = (bf16[32,640]{1,0:T(8,128)(2,1)}, bf16[32,640]{1,0:T(8,128)(2,1)S(1)}, u32[]{:S(2)}, u32[]{:S(2)}) collective-permute-start(bf16[32,640]{1,0:T(8,128)(2,1)} %bitcast.10), channel_id=1, source_target_pairs={{0,12},{2,14},{4,8},{6,10},{8,4},{10,6},{12,0},{14,2},{1,13},{3,15... | collective-permute-start | bytes 122888 | tf_op jit(solution)/shard_map/ppermute | solution.py:31
  5.8 7.5 %collective-permute-start = (bf16[32,640]{1,0:T(8,128)(2,1)}, bf16[32,640]{1,0:T(8,128)(2,1)S(1)}, u32[]{:S(2)}, u32[]{:S(2)}) collective-permute-start(bf16[32,640]{1,0:T(8,128)(2,1)} %bitcast.11), channel_id=1, source_target_pairs={{0,2},{2,0},{4,6},{6,4},{8,10},{10,8},{12,14},{14,12},{1,3},{3,1},... | collective-permute-start | bytes 122888 | tf_op jit(solution)/shard_map/ppermute | solution.py:31
  7.5 10.0 %copy-start = (bf16[10,40,512]{2,1,0:T(8,128)(2,1)S(1)}, bf16[10,40,512]{2,1,0:T(8,128)(2,1)}, u32[]{:S(2)}) copy-start(bf16[10,40,512]{2,1,0:T(8,128)(2,1)} %refs_5_.5) | copy-start | bytes 1228804
  7.5 5.8 %collective-permute-start.2 = (bf16[32,640]{1,0:T(8,128)(2,1)S(1)}, bf16[32,640]{1,0:T(8,128)(2,1)S(1)}, u32[]{:S(2)}, u32[]{:S(2)}) collective-permute-start(bf16[32,640]{1,0:T(8,128)(2,1)S(1)} %shard_map.73.refs_3_), channel_id=1, source_target_pairs={{0,2},{2,0},{4,6},{6,4},{8,10},{10,8},{12,14},{14,12},{1,3},{3,1},... | collective-permute-start | bytes 122888 | tf_op jit(solution)/shard_map/ppermute | solution.py:31
  9.1 4.4 %collective-permute-start.4 = (bf16[32,640]{1,0:T(8,128)(2,1)S(1)}, bf16[32,640]{1,0:T(8,128)(2,1)S(1)}, u32[]{:S(2)}, u32[]{:S(2)}) collective-permute-start(bf16[32,640]{1,0:T(8,128)(2,1)S(1)} %collective-permute-done.3.refs_5_), channel_id=1, source_target_pairs={{0,2},{2,0},{4,6},{6,4},{8,10},{10,8},{12,14},{14,12},{1,3},{3,1},... | collective-permute-start | bytes 122888 | tf_op jit(solution)/shard_map/ppermute | solution.py:31
  11.8 4.0 %collective-permute-start.6 = (bf16[32,640]{1,0:T(8,128)(2,1)S(1)}, bf16[32,640]{1,0:T(8,128)(2,1)S(1)}, u32[]{:S(2)}, u32[]{:S(2)}) collective-permute-start(bf16[32,640]{1,0:T(8,128)(2,1)S(1)} %collective-permute-done.5.refs_7_), channel_id=1, source_target_pairs={{0,2},{2,0},{4,6},{6,4},{8,10},{10,8},{12,14},{14,12},{1,3},{3,1},... | collective-permute-start | bytes 122888 | tf_op jit(solution)/shard_map/ppermute | solution.py:31
  15.8 1.7 %collective-permute-start.7 = (bf16[8,32,640]{2,1,0:T(8,128)(2,1)S(1)}, bf16[8,32,640]{2,1,0:T(8,128)(2,1)S(1)}, u32[]{:S(2)}, u32[]{:S(2)}) collective-permute-start(bf16[8,32,640]{2,1,0:T(8,128)(2,1)S(1)} %shard_map.74.refs_0_), channel_id=1, source_target_pairs={{0,1},{1,0},{2,3},{3,2},{4,5},{5,4},{6,7},{7,6},{8,9},{9,8},{10,11... | collective-permute-start | bytes 983048 | tf_op jit(solution)/shard_map/ppermute | solution.py:31
  16.8 7.9 %copy-start.1 = (f32[10,512]{1,0:T(8,128)S(1)}, f32[10,512]{1,0:T(8,128)}, u32[]{:S(2)}) copy-start(f32[10,512]{1,0:T(8,128)} %refs_6_.1) | copy-start | bytes 61444
  16.9 7.9 %copy-start.3 = (s32[10]{0:T(128)S(1)}, s32[10]{0:T(128)}, u32[]{:S(2)}) copy-start(s32[10]{0:T(128)} %refs_0_.7) | copy-start | bytes 124
  19.3 5.4 %collective-permute-start.10 = (bf16[3,32,512]{2,1,0:T(8,128)(2,1)S(1)}, bf16[3,32,512]{2,1,0:T(8,128)(2,1)S(1)}, u32[]{:S(2)}, u32[]{:S(2)}) collective-permute-start(bf16[3,32,512]{2,1,0:T(8,128)(2,1)S(1)} %get-tuple-element.26), channel_id=1, source_target_pairs={{0,16},{16,0},{1,17},{17,1},{2,18},{18,2},{3,19},{19,3},{4,20},{20... | collective-permute-start | bytes 294920 | tf_op jit(solution)/shard_map/ppermute | solution.py:31
  21.7 4.7 %collective-permute-start.9 = (bf16[2,32,512]{2,1,0:T(8,128)(2,1)S(1)}, bf16[2,32,512]{2,1,0:T(8,128)(2,1)S(1)}, u32[]{:S(2)}, u32[]{:S(2)}) collective-permute-start(bf16[2,32,512]{2,1,0:T(8,128)(2,1)S(1)} %get-tuple-element.23.refs_2_), channel_id=1, source_target_pairs={{0,16},{16,0},{1,17},{17,1},{2,18},{18,2},{3,19},{19,3},{4,20},{20... | collective-permute-start | bytes 196616 | tf_op jit(solution)/shard_map/ppermute | solution.py:31
  23.2 4.3 %collective-permute-start.8 = (f32[32,256]{1,0:T(8,128)S(1)}, f32[32,256]{1,0:T(8,128)S(1)}, u32[]{:S(2)}, u32[]{:S(2)}) collective-permute-start(f32[32,256]{1,0:T(8,128)S(1)} %shard_map.78.refs_6_.refs_0_), channel_id=1, source_target_pairs={{0,16},{16,0},{1,17},{17,1},{2,18},{18,2},{3,19},{19,3},{4,20},{20... | collective-permute-start | bytes 98312 | tf_op jit(solution)/shard_map/ppermute | solution.py:31
  28.0 14.2 %copy-start.4 = (f32[640]{0:T(1024)S(1)}, f32[640]{0:T(1024)}, u32[]{:S(2)}) copy-start(f32[640]{0:T(1024)} %param.8) | copy-start | bytes 7684
  28.1 1.6 %collective-permute-start.11 = (bf16[4,32,640]{2,1,0:T(8,128)(2,1)S(1)}, bf16[4,32,640]{2,1,0:T(8,128)(2,1)S(1)}, u32[]{:S(2)}, u32[]{:S(2)}) collective-permute-start(bf16[4,32,640]{2,1,0:T(8,128)(2,1)S(1)} %get-tuple-element.28), channel_id=1, source_target_pairs={{0,1},{1,0},{2,3},{3,2},{4,5},{5,4},{6,7},{7,6},{8,9},{9,8},{10,11... | collective-permute-start | bytes 491528 | tf_op jit(solution)/shard_map/ppermute | solution.py:31
  30.3 2.1 %collective-permute-start.15 = (bf16[4,32,640]{2,1,0:T(8,128)(2,1)S(1)}, bf16[4,32,640]{2,1,0:T(8,128)(2,1)S(1)}, u32[]{:S(2)}, u32[]{:S(2)}) collective-permute-start(bf16[4,32,640]{2,1,0:T(8,128)(2,1)S(1)} %get-tuple-element.34), channel_id=1, source_target_pairs={{0,1},{1,0},{2,3},{3,2},{4,5},{5,4},{6,7},{7,6},{8,9},{9,8},{10,11... | collective-permute-start | bytes 491528 | tf_op jit(solution)/shard_map/ppermute | solution.py:31
  30.9 4.8 %collective-permute-start.12 = (bf16[2,32,640]{2,1,0:T(8,128)(2,1)S(1)}, bf16[2,32,640]{2,1,0:T(8,128)(2,1)S(1)}, u32[]{:S(2)}, u32[]{:S(2)}) collective-permute-start(bf16[2,32,640]{2,1,0:T(8,128)(2,1)S(1)} %get-tuple-element.30), channel_id=1, source_target_pairs={{0,2},{2,0},{4,6},{6,4},{8,10},{10,8},{12,14},{14,12},{1,3},{3,1},... | collective-permute-start | bytes 245768 | tf_op jit(solution)/shard_map/ppermute | solution.py:31
  32.4 4.8 %collective-permute-start.16 = (bf16[2,32,640]{2,1,0:T(8,128)(2,1)S(1)}, bf16[2,32,640]{2,1,0:T(8,128)(2,1)S(1)}, u32[]{:S(2)}, u32[]{:S(2)}) collective-permute-start(bf16[2,32,640]{2,1,0:T(8,128)(2,1)S(1)} %get-tuple-element.36), channel_id=1, source_target_pairs={{0,2},{2,0},{4,6},{6,4},{8,10},{10,8},{12,14},{14,12},{1,3},{3,1},... | collective-permute-start | bytes 245768 | tf_op jit(solution)/shard_map/ppermute | solution.py:31
  35.7 5.0 %collective-permute-start.13 = (bf16[32,640]{1,0:T(8,128)(2,1)S(1)}, bf16[32,640]{1,0:T(8,128)(2,1)S(1)}, u32[]{:S(2)}, u32[]{:S(2)}) collective-permute-start(bf16[32,640]{1,0:T(8,128)(2,1)S(1)} %get-tuple-element.31), channel_id=1, source_target_pairs={{0,8},{2,10},{4,12},{6,14},{8,0},{10,2},{12,4},{14,6},{1,9},{3,11}... | collective-permute-start | bytes 122888 | tf_op jit(solution)/shard_map/ppermute | solution.py:31
  36.5 5.8 %collective-permute-start.14 = (bf16[32,640]{1,0:T(8,128)(2,1)S(1)}, bf16[32,640]{1,0:T(8,128)(2,1)S(1)}, u32[]{:S(2)}, u32[]{:S(2)}) collective-permute-start(bf16[32,640]{1,0:T(8,128)(2,1)S(1)} %get-tuple-element.32), channel_id=1, source_target_pairs={{0,12},{2,14},{4,8},{6,10},{8,4},{10,6},{12,0},{14,2},{1,13},{3,15... | collective-permute-start | bytes 122888 | tf_op jit(solution)/shard_map/ppermute | solution.py:31
  37.3 5.0 %collective-permute-start.17 = (bf16[32,640]{1,0:T(8,128)(2,1)S(1)}, bf16[32,640]{1,0:T(8,128)(2,1)S(1)}, u32[]{:S(2)}, u32[]{:S(2)}) collective-permute-start(bf16[32,640]{1,0:T(8,128)(2,1)S(1)} %get-tuple-element.38), channel_id=1, source_target_pairs={{0,4},{2,6},{4,0},{6,2},{8,12},{10,14},{12,8},{14,10},{1,5},{3,7},... | collective-permute-start | bytes 122888 | tf_op jit(solution)/shard_map/ppermute | solution.py:31
